TPU v7x, 128 devices: a whole 4x4x4 slice. The times are simulated.
128 devices in a mesh: dp: 2 (over core), fsdp: 64 (over z, y, x).
Axes of the slice: x: 4, y: 4, z: 4, core: 2. Of those that a mesh axis runs over, the one named last changes fastest.
Arguments:
- master: float32 [1, 13075328], P(None, ('dp', 'fsdp'))
- adam_m: float32 [1, 13075328], P(None, ('dp', 'fsdp'))
- adam_v: float32 [1, 13075328], P(None, ('dp', 'fsdp'))
- inputs: bfloat16 [1, 512, 256, 896], P(None, ('dp', 'fsdp'))
- targets: bfloat16 [1, 512, 256, 896], P(None, ('dp', 'fsdp'))
Outputs:
- output 1: float32 [1, 13075328], P(None, ('dp', 'fsdp'))
- output 2: float32 [1, 13075328], P(None, ('dp', 'fsdp'))
- output 3: float32 [1, 13075328], P(None, ('dp', 'fsdp'))
- output 4: float32 [], replicated
All inputs are finite; a program needn't handle non-finite values.
Results may differ from a plain program's by a relative error of at most 0.001.
Values are sent between devices in bfloat16 or wider.
A program may use at most 1 GiB of HBM per device.

v0:
```python
import jax
import jax.numpy as jnp
from jax import lax
from jax.sharding import PartitionSpec as P

ADAM_STEP = 3
LEARN_RATE = 2e-3
BETA_ONE = 0.9
BETA_TWO = 0.999
ADAM_EPS = 1e-8
DECAY_RATE = 0.1
RMS_EPS = 1e-5


def unpack_layer(flat_work, dmodel, hidden_ff):
    split_at = dmodel + 2 * dmodel * hidden_ff
    gain_vec = flat_work[:dmodel]
    w_gu = flat_work[dmodel:split_at].reshape(2, dmodel, hidden_ff)
    w_two = flat_work[split_at:].reshape(hidden_ff, dmodel)
    return gain_vec, w_gu, w_two


def layer_forward(hidden, layer_w):
    gain_vec, w_gu, w_two = layer_w
    inv_rms = lax.rsqrt(jnp.mean(hidden * hidden, axis=-1, keepdims=True) + RMS_EPS)
    normed = (hidden * inv_rms * gain_vec.astype(jnp.float32)).astype(jnp.bfloat16)
    gate_up = jnp.einsum('td,kdf->tkf', normed, w_gu, preferred_element_type=jnp.float32)
    inner = (jax.nn.silu(gate_up[:, 0]) * gate_up[:, 1]).astype(jnp.bfloat16)
    new_hidden = hidden + jnp.dot(inner, w_two, preferred_element_type=jnp.float32)
    return new_hidden, gate_up


def layer_backward(grad_h, hidden, gate_up, layer_w):
    gain_vec, w_gu, w_two = layer_w
    inv_rms = lax.rsqrt(jnp.mean(hidden * hidden, axis=-1, keepdims=True) + RMS_EPS)
    normed_f = hidden * inv_rms
    gain_f = gain_vec.astype(jnp.float32)
    normed = (normed_f * gain_f).astype(jnp.bfloat16)
    gate_pre = gate_up[:, 0]
    up_pre = gate_up[:, 1]
    sigmoid_g = jax.nn.sigmoid(gate_pre)
    silu_g = gate_pre * sigmoid_g
    inner = (silu_g * up_pre).astype(jnp.bfloat16)
    grad_hb = grad_h.astype(jnp.bfloat16)
    d_two = jnp.einsum('tf,td->fd', inner, grad_hb, preferred_element_type=jnp.float32)
    d_inner = jnp.einsum('td,fd->tf', grad_hb, w_two, preferred_element_type=jnp.float32)
    d_gate = d_inner * up_pre * sigmoid_g * (1.0 + gate_pre * (1.0 - sigmoid_g))
    d_gu = jnp.stack([d_gate, d_inner * silu_g], axis=1).astype(jnp.bfloat16)
    d_wgu = jnp.einsum('td,tkf->kdf', normed, d_gu, preferred_element_type=jnp.float32)
    d_normed = jnp.einsum('tkf,kdf->td', d_gu, w_gu, preferred_element_type=jnp.float32)
    d_gain = jnp.sum(d_normed * normed_f, axis=0)
    d_hn = d_normed * gain_f
    grad_prev = grad_h + inv_rms * (d_hn - normed_f * jnp.mean(d_hn * normed_f, axis=-1, keepdims=True))
    flat_grad = jnp.concatenate([d_gain, d_wgu.reshape(-1), d_two.reshape(-1)])
    return grad_prev, flat_grad


def adam_update(master, adam_m, adam_v, grad_mean):
    m_new = BETA_ONE * adam_m + (1.0 - BETA_ONE) * grad_mean
    v_new = BETA_TWO * adam_v + (1.0 - BETA_TWO) * grad_mean * grad_mean
    m_hat = m_new / (1.0 - BETA_ONE ** ADAM_STEP)
    v_hat = v_new / (1.0 - BETA_TWO ** ADAM_STEP)
    master_new = master - LEARN_RATE * (m_hat / (jnp.sqrt(v_hat) + ADAM_EPS) + DECAY_RATE * master)
    return master_new, m_new, v_new


def solution(mesh):
    rep_size = mesh.shape['dp']
    grp_size = mesh.shape['fsdp']
    flat_spec = P(None, ('dp', 'fsdp'))
    act_spec = P(None, ('dp', 'fsdp'), None, None)

    def train_step(master, adam_m, adam_v, inputs, targets):
        micro_count, batch, seq_len, dmodel = inputs.shape
        layers, flat_len = master.shape
        hidden_ff = (flat_len // dmodel - 1) // 3
        shard_len = flat_len // (rep_size * grp_size)
        token_total = micro_count * batch * seq_len

        def local_step(master_sh, m_sh, v_sh, x_loc, y_loc):
            tok_local = x_loc.shape[1] * x_loc.shape[2]
            x_tok = x_loc.reshape(micro_count, tok_local, dmodel)
            y_tok = y_loc.reshape(micro_count, tok_local, dmodel)
            rep_work = lax.all_gather(master_sh.astype(jnp.bfloat16), 'dp', axis=1)

            def micro_step(carry, mb_pair):
                loss_acc, grad_accs = carry
                x_mb, y_mb = mb_pair
                hidden = x_mb.astype(jnp.float32)
                saved_acts = []
                for layer_idx in range(layers):
                    flat_work = lax.all_gather(rep_work[layer_idx], 'fsdp', axis=1).reshape(flat_len)
                    layer_w = unpack_layer(flat_work, dmodel, hidden_ff)
                    new_hidden, gate_up = layer_forward(hidden, layer_w)
                    saved_acts.append((hidden, gate_up, layer_w))
                    hidden = new_hidden
                residual_err = hidden - y_mb.astype(jnp.float32)
                loss_acc = loss_acc + 0.5 * jnp.sum(residual_err * residual_err)
                grad_h = residual_err
                new_accs = list(grad_accs)
                for layer_idx in reversed(range(layers)):
                    hidden_in, gate_up, layer_w = saved_acts[layer_idx]
                    grad_h, flat_grad = layer_backward(grad_h, hidden_in, gate_up, layer_w)
                    group_part = lax.psum_scatter(flat_grad.reshape(rep_size, grp_size, shard_len), 'fsdp', scatter_dimension=1, tiled=False)
                    new_accs[layer_idx] = grad_accs[layer_idx] + group_part
                return (loss_acc, tuple(new_accs)), None

            init_accs = tuple(jnp.zeros((rep_size, shard_len), jnp.float32) for layer_idx in range(layers))
            (loss_sum, grad_accs), scan_ys = lax.scan(micro_step, (jnp.zeros((), jnp.float32), init_accs), (x_tok, y_tok))
            grad_mean = jnp.stack([lax.psum_scatter(acc_layer, 'dp', scatter_dimension=0, tiled=False) for acc_layer in grad_accs]) / token_total
            loss_value = lax.psum(loss_sum, ('dp', 'fsdp')) / token_total
            master_new, m_new, v_new = adam_update(master_sh, m_sh, v_sh, grad_mean)
            return master_new, m_new, v_new, loss_value

        return jax.shard_map(local_step, mesh=mesh, in_specs=(flat_spec, flat_spec, flat_spec, act_spec, act_spec), out_specs=(flat_spec, flat_spec, flat_spec, P()), check_vma=False)(master, adam_m, adam_v, inputs, targets)

    return train_step
```

profile of v0, /device:TPU:1, one launch (start us, length us, event | category | flops | bytes accessed | tf_op | source)
XLA Modules:
  0.0 1437.7 jit_solution(4828384905155287513)
XLA Ops:
  7.2 0.0 all-gather.6.cloned.1.call-start
  7.2 1.3 convert_bitcast_fusion
  8.5 3.4 all-gather.2
  11.9 1.2 copy.22
  13.0 0.0 all-gather.6.cloned.1.call-update
  13.1 0.0 all-reduce.5.cloned.1.call-start
  13.1 1.9 fusion.11
  15.1 0.6 copy.19
  15.7 134.5 %all-gather.6.cloned.1.call-done = bf16[64,102151,2]{1,2,0:T(2,128)(2,1)} async-done(((bf16[1,102151,2]{1,2,0:T(2,128)(2,1)}), bf16[64,102151,2]{1,2,0:T(2,128)(2,1)}) %all-gather.6.cloned.1.call-update) | async-done | bytes 26150672 | tf_op jit(solution)/shard_map/while/body/eval_jaxpr/all_gather | solution.py:92
  150.2 18.2 %copy.23 = bf16[64,102151,2]{1,0,2:T(8,128)(2,1)} copy(bf16[64,102151,2]{1,2,0:T(2,128)(2,1)} %all-gather.6.cloned.1.call-done) | data formatting | bytes 52301312 | tf_op jit(solution)/shard_map/while/body/eval_jaxpr/all_gather | solution.py:92
  168.4 60.6 %reshape.91 = bf16[13075328]{0:T(1024)(128)(2,1)} reshape(bf16[2,64,102151]{2,1,0:T(8,128)(2,1)} %bitcast.80) | data formatting | bytes 52301312
  228.9 38.5 %reshape.92 = bf16[2,6537664]{1,0:T(2,128)(2,1)} reshape(bf16[13075328]{0:T(1024)(128)(2,1)} %reshape.91) | data formatting | bytes 52301312
  267.4 21.6 %bitcast_bitcast_fusion = bf16[2,6537664]{1,0:T(2,128)(2,1)} fusion(bf16[2,6537664]{1,0:T(2,128)(2,1)} %reshape.92), kind=kLoop, calls=%fused_computation.46 | loop fusion | bytes 52301312
  289.0 72.6 %reshape.71 = bf16[13075328]{0:T(1024)(128)(2,1)} reshape(bf16[2,6537664]{1,0:T(2,128)(2,1)} %bitcast_bitcast_fusion) | data formatting | bytes 52301312 | tf_op jit(solution)/shard_map/while/body/eval_jaxpr/reshape | solution.py:92
  361.6 0.7 slice_convert_fusion
  362.3 12.9 slice.32
  375.2 46.5 %slice.29 = bf16[14593,896]{1,0:T(8,128)(2,1)} reshape(bf16[13075328]{0:T(1024)(128)(2,1)} %reshape.71) | data formatting | bytes 52301312 | tf_op jit(solution)/shard_map/while/body/eval_jaxpr/slice | solution.py:19
  421.7 0.0 copy-start
  421.7 31.7 %reshape.72 = bf16[2,896,4864]{2,1,0:T(8,128)(2,1)} reshape(bf16[8716288]{0:T(1024)(128)(2,1)} %slice.32) | data formatting | bytes 34865152 | tf_op jit(solution)/shard_map/while/body/eval_jaxpr/reshape | solution.py:18
  453.4 0.0 copy-done
  453.4 0.5 fusion.13
  453.9 28.9 %fusion.27 = f32[1024,2,4864]{2,0,1:T(8,128)} fusion(bf16[1024,896,1]{1,0,2:T(8,128)(2,1)S(1)} %bitcast.81, bf16[2,896,4864]{2,1,0:T(8,128)(2,1)} %reshape.72), kind=kOutput, calls=%fused_computation.47 | convolution fusion | flops 17850957824 | bytes 59113472 | tf_op jit(solution)/shard_map/while/body/eval_jaxpr/td,kdf->tkf/dot_general | solution.py:27
  482.7 0.0 copy-start.7
  482.7 14.0 multiply_convert_fusion.2
  496.8 0.0 copy-start.1
  496.8 0.0 copy-done.7
  496.8 19.0 %multiply_reduce_fusion = (f32[]{:T(128)}, bf16[1024,896]{1,0:T(8,128)(2,1)}) fusion(bf16[1024,896]{1,0:T(8,128)(2,1)S(1)} %bitcast.85, bf16[1024,4864]{1,0:T(8,128)(2,1)S(1)} %multiply_convert_fusion.2, bf16[14593,896]{1,0:T(8,128)(2,1)} %slice.29, bf16[1,4,256,896]{3,2,1,0:T(8,128)(2,1)S(1)} %copy-done), kind=kOutput, calls=%fused_computation.29 | convolution fusion | flops 8931901440 | bytes 24182788 | tf_op jit(solution)/shard_map/while/body/eval_jaxpr/dot_general | solution.py:29
  515.8 0.0 copy-done.1
  515.8 29.6 %fusion.3 = (bf16[1024,1,4864]{2,0,1:T(8,128)(2,1)}, bf16[1024,1,4864]{2,0,1:T(8,128)(2,1)}) fusion(f32[1024,2,4864]{2,0,1:T(8,128)} %fusion.27, bf16[14593,896]{1,0:T(8,128)(2,1)} %slice.29, bf16[1024,896]{1,0:T(8,128)(2,1)} %get-tuple-element.30), kind=kOutput, calls=%fused_computation.12 | convolution fusion | flops 8990228480 | bytes 70320128 | tf_op jit(solution)/shard_map/while/body/eval_jaxpr/td,fd->tf/dot_general | solution.py:46
  545.4 0.0 copy-start.6
  545.4 17.3 %fusion.17 = f32[4864,896]{1,0:T(8,128)} fusion(bf16[1024,4864]{1,0:T(8,128)(2,1)} %copy-done.1, bf16[1024,896]{1,0:T(8,128)(2,1)} %get-tuple-element.30), kind=kOutput, calls=%fused_computation.31 | convolution fusion | flops 8925478912 | bytes 29229056 | tf_op jit(solution)/shard_map/while/body/eval_jaxpr/tf,td->fd/dot_general | solution.py:45
  562.7 0.0 copy-done.6
  562.7 1.7 fusion.10
  564.4 18.5 %reshape.74 = f32[4358144]{0:T(1024)} reshape(f32[4864,896]{1,0:T(8,128)} %fusion.17) | data formatting | bytes 34865152 | tf_op jit(solution)/shard_map/while/body/eval_jaxpr/reshape | solution.py:54
  582.9 0.0 copy-start.2
  582.9 26.7 %fusion.8 = f32[896]{0:T(1024)S(1)} fusion(bf16[1,4,256,896]{3,2,1,0:T(8,128)(2,1)S(1)} %copy-done, bf16[2,896,4864]{2,1,0:T(8,128)(2,1)} %reshape.72, bf16[1024,1,4864]{2,0,1:T(8,128)(2,1)} %get-tuple-element.26, bf16[1024,1,4864]{2,0,1:T(8,128)(2,1)} %get-tuple-element.25, f32[1024]{0:T(1024)S(1)} %bitcast.84), kind=kOutput, calls=%fused_computation.19 | convolution fusion | flops 17864589312 | bytes 39198208 | tf_op jit(solution)/shard_map/while/body/eval_jaxpr/tkf,kdf->td/dot_general | solution.py:50
  609.6 0.0 copy-done.2
  609.7 29.3 %convolution_bitcast_fusion = f32[2,896,4864]{1,2,0:T(8,128)} fusion(bf16[1024,1,4864]{2,0,1:T(8,128)(2,1)} %get-tuple-element.26, bf16[1024,1,4864]{2,0,1:T(8,128)(2,1)} %get-tuple-element.25, bf16[1024,896]{1,0:T(8,128)(2,1)S(1)} %copy-done.2), kind=kOutput, calls=%fused_computation.9 | convolution fusion | flops 17860919296 | bytes 56623104 | tf_op jit(solution)/shard_map/while/body/eval_jaxpr/td,tkf->kdf/dot_general | solution.py:49
  639.0 33.9 %copy.15 = f32[2,896,4864]{2,1,0:T(8,128)} copy(f32[2,896,4864]{1,2,0:T(8,128)} %convolution_bitcast_fusion) | data formatting | bytes 69730304 | tf_op jit(solution)/shard_map/while/body/eval_jaxpr/td,tkf->kdf/transpose | solution.py:49
  672.9 35.0 %reshape.73 = f32[8716288]{0:T(1024)} reshape(f32[2,896,4864]{2,1,0:T(8,128)} %copy.15) | data formatting | bytes 69730304 | tf_op jit(solution)/shard_map/while/body/eval_jaxpr/reshape | solution.py:54
  707.9 36.0 %pad_maximum_fusion = f32[13075328]{0:T(1024)} fusion(f32[4358144]{0:T(1024)} %reshape.74, f32[8716288]{0:T(1024)} %reshape.73, f32[896]{0:T(1024)S(1)} %fusion.8), kind=kLoop, calls=%fused_computation | loop fusion | flops 26150656 | bytes 104602624 | tf_op jit(solution)/shard_map/while/body/eval_jaxpr/concatenate | solution.py:54
  743.9 70.4 %reshape.75 = f32[2,64,102151]{2,1,0:T(8,128)} reshape(f32[13075328]{0:T(1024)} %pad_maximum_fusion) | data formatting | bytes 104602624 | tf_op jit(solution)/shard_map/while/body/eval_jaxpr/reshape | solution.py:104
  814.3 85.4 %copy.16 = f32[2,64,102151]{2,0,1:T(2,128)} copy(f32[2,64,102151]{2,1,0:T(8,128)} %reshape.75) | data formatting | bytes 104602624 | tf_op jit(solution)/shard_map/while/body/eval_jaxpr/reshape | solution.py:104
  899.7 0.0 copy-start.9
  899.7 0.0 copy-start.8
  899.7 0.0 copy-start.3
  899.7 0.0 copy-start.4
  899.7 0.0 copy-start.5
  899.7 0.0 all-reduce.5.cloned.1.call-update
  899.7 0.0 all-reduce.7.cloned.1.call-start
  899.8 0.5 copy-done.9
  900.3 0.6 dynamic-slice
  900.9 452.3 %all-reduce.5.cloned.1.call-done = f32[2,64,102151]{2,0,1:T(2,128)} async-done(((f32[2,64,102151]{2,0,1:T(2,128)}), f32[2,64,102151]{2,0,1:T(2,128)}) %all-reduce.5.cloned.1.call-update) | async-done | bytes 52301328
  1353.3 2.7 dynamic-slice_bitcast_fusion
  1356.0 0.0 all-reduce.7.cloned.1.call-update
  1356.7 0.0 copy-done.8
  1356.7 0.7 dynamic-slice.2
  1357.3 66.2 %psum.7 = f32[]{:T(128)} all-reduce(f32[]{:T(128)S(6)} %mul.156), channel_id=1, replica_groups=mesh['dp'=2,'fsdp'=64] {'dp','fsdp'}, use_global_device_ids=true, to_apply=%region_5.6 | all-reduce | flops 1 | bytes 8 | tf_op jit(solution)/shard_map/psum | solution.py:111
  1424.2 0.0 all-reduce.7.cloned.1.call-done
  1424.2 0.0 copy-done.3
  1424.2 0.0 copy-done.4
  1424.2 0.0 copy-done.5
  1424.2 5.4 multiply_subtract_fusion
  (1 shorter events, 0.0 us)
Async XLA Ops:
  7.2 143.0 %all-gather.6.cloned.1.call-start = ((), (), s32[]{:S(2)}) async-start(), calls=%async_computation | async-start | bytes 26590720 | tf_op jit(solution)/shard_map/while/body/eval_jaxpr/all_gather | solution.py:92
  13.1 1340.2 %all-reduce.5.cloned.1.call-start = ((), (), s32[]{:S(2)}) async-start(), calls=%async_computation.1 | async-start | bytes 104726528
  421.7 31.7 %copy-start = (bf16[1,4,256,896]{3,2,1,0:T(8,128)(2,1)S(1)}, bf16[1,4,256,896]{3,2,1,0:T(8,128)(2,1)}, u32[]{:S(2)}) copy-start(bf16[1,4,256,896]{3,2,1,0:T(8,128)(2,1)} %param.8) | copy-start | bytes 5505028
  482.7 14.1 copy-start.7
  496.8 19.0 %copy-start.1 = (bf16[1024,4864]{1,0:T(8,128)(2,1)}, bf16[1024,4864]{1,0:T(8,128)(2,1)S(1)}, u32[]{:S(2)}) copy-start(bf16[1024,4864]{1,0:T(8,128)(2,1)S(1)} %multiply_convert_fusion.2) | copy-start | bytes 29884420
  545.4 17.3 %copy-start.6 = (f32[1,2,4,128]{3,1,2,0:T(2,128)S(1)}, f32[1,2,4,128]{3,1,2,0:T(2,128)}, u32[]{:S(2)}) copy-start(f32[1,2,4,128]{3,1,2,0:T(2,128)} %copy.19) | copy-start | bytes 12292
  582.9 26.7 %copy-start.2 = (bf16[1024,896]{1,0:T(8,128)(2,1)S(1)}, bf16[1024,896]{1,0:T(8,128)(2,1)}, u32[]{:S(2)}) copy-start(bf16[1024,896]{1,0:T(8,128)(2,1)} %fusion.10) | copy-start | bytes 5505028
  899.7 0.7 copy-start.9
  899.7 457.0 %copy-start.8 = (u32[128]{0:T(128)S(1)}, u32[128]{0:T(128)}, u32[]{:S(2)}) copy-start(u32[128]{0:T(128)} %constant.65) | copy-start | bytes 1540
  899.7 524.5 %copy-start.3 = (f32[1,102151]{1,0:T(1,128)S(1)}, f32[1,102151]{1,0:T(1,128)}, u32[]{:S(2)}) copy-start(f32[1,102151]{1,0:T(1,128)} %param.5) | copy-start | bytes 1225816
  899.7 524.5 %copy-start.4 = (f32[1,102151]{1,0:T(1,128)S(1)}, f32[1,102151]{1,0:T(1,128)}, u32[]{:S(2)}) copy-start(f32[1,102151]{1,0:T(1,128)} %param.6) | copy-start | bytes 1225816
  899.7 524.5 %copy-start.5 = (f32[1,102151]{1,0:T(1,128)S(1)}, f32[1,102151]{1,0:T(1,128)}, u32[]{:S(2)}) copy-start(f32[1,102151]{1,0:T(1,128)} %param.7) | copy-start | bytes 1225816
  899.7 524.5 %all-reduce.7.cloned.1.call-start = ((), (), s32[]{:S(2)}) async-start(), calls=%async_computation.2 | async-start | bytes 1636352
Sparse Core Ops, SparseCore 0:
  13.2 136.9 all-gather.5
  899.9 453.3 all-reduce.4
  1356.1 26.6 all-reduce.6
where the time goes:
time: 1450 us; the launch traced here: 1440 us
  waiting for transfers between devices  587 us (40%)
  local copies, waits for them, and re-layouts  552 us (38%)
  matrix products  151 us (10%)
  blocking collectives  69.6 us (5%)
  other arithmetic  61.5 us (4%)
  between operations  16.8 us (1%)
    unnamed x5, waiting for transfers between devices  452 us
    reshape x2, local copies, waits for them, and re-layouts, micro_step(): flat_grad.reshape(rep_size, grp_size, shard_len)  156 us
    all_gather x1, waiting for transfers between devices, micro_step(): lax.all_gather(rep_work[layer_idx], 'fsdp', axis=1).reshape(flat_len)  134 us
    unnamed x27, local copies, waits for them, and re-layouts  124 us
    reshape x1, local copies, waits for them, and re-layouts, micro_step(): lax.all_gather(rep_work[layer_idx], 'fsdp', axis=1).reshape(flat_len)  72.6 us
    psum x1, blocking collectives, local_step(): loss_value = lax.psum(loss_sum, ('dp', 'fsdp')) / token_total  66.2 us
    reshape x2, local copies, waits for them, and re-layouts, layer_backward(): flat_grad = jnp.concatenate([d_gain, d_wgu.reshape(-1), d_two.reshape(-1)])  53.5 us
    slice x1, local copies, waits for them, and re-layouts, unpack_layer(): w_two = flat_work[split_at:].reshape(hidden_ff, dmodel)  46.5 us
  transfers between devices with their start and end apart: 3, of which 2 were waited for; matrix products, arithmetic and copies ran while one was open for 0% of the time, Pallas kernels for 0%

commit v1 on v0

v1 whole, which is shorter than its diff:
```python
import functools

import jax
import jax.numpy as jnp
from jax import lax
from jax.experimental import pallas as pl
from jax.experimental.pallas import tpu as pltpu
from jax.sharding import PartitionSpec as P

ADAM_STEP = 3
LEARN_RATE = 2e-3
BETA_ONE = 0.9
BETA_TWO = 0.999
ADAM_EPS = 1e-8
DECAY_RATE = 0.1
RMS_EPS = 1e-5

D = 896
FF = 4864
FLAT = D * (3 * FF + 1)
NDEV = 128
GRP = 64
SHARD = FLAT // NDEV
NB = FF // 128
ND = D // 128
HB = NB // 2
W2_START = D + 2 * D * FF
FIRST_W2 = 85
SPILL = 35840
ROWS13, ROWS2 = 24, 120
AL_LEN = ROWS13 * FF

CHUNKS = (3, 8, 8)
OFFS = (0, 3, 11)
TPD = (16, 42, 42)
SLOT0 = (0, 16, 58)
SLOTS = 100
GAIN_F = GRP - 1

MESH = pl.DeviceIdType.MESH


def row_start(dev):
    return (21 * dev + 7) // 8


def w2_row_start(dev):
    return jnp.maximum((114 * dev - 9728 + 7) // 8, 0)


def tile_of(k, c, p):
    n = CHUNKS[k]
    row13 = p // n
    col13 = HB * c + OFFS[k] + p % n
    p2 = p - 2 * (D // 8) * n
    row2 = (FF // 16) * c + 16 * OFFS[k] + p2 // ND
    col2 = p2 % ND
    return row13, col13, row2, col2


def my_index():
    return lax.axis_index('dp') * GRP + lax.axis_index('fsdp')


def move(src, dst, send_sem, recv_sem, c, f, waiting):
    stays = (c == lax.axis_index('dp')) & (f == lax.axis_index('fsdp'))

    def remote():
        return pltpu.make_async_remote_copy(
            src_ref=src, dst_ref=dst, send_sem=send_sem, recv_sem=recv_sem, device_id=(c, f), device_id_type=MESH)

    if waiting:
        @pl.when(jnp.logical_not(stays))
        def _():
            remote().wait_send()
    else:
        @pl.when(jnp.logical_not(stays))
        def _():
            remote().start()

        @pl.when(stays)
        def _():
            pltpu.make_async_copy(src, dst, recv_sem).start()


def spread_kernel(src13, src2, gain_src, out, send13, send2, send_gain, recv):
    dev = my_index()
    me_f = lax.axis_index('fsdp')

    def all_sends(waiting):
        def send(src, k, c, p, sem):
            move(src, out.at[SLOT0[k] + p % TPD[k]], sem, recv.at[k], c, p // TPD[k], waiting)

        @pl.when(dev < FIRST_W2)
        def _():
            first = row_start(dev)

            def per_row(t, carry):
                for k in range(len(CHUNKS)):
                    n = CHUNKS[k]

                    def per_col(j, carry2):
                        for c in range(2):
                            col = HB * c + OFFS[k] + j
                            send(src13.at[pl.ds(t * 8, 8), col], k, c, (first + t) * n + j, send13.at[t])
                        return carry2

                    lax.fori_loop(0, n, per_col, 0)
                return carry

            lax.fori_loop(0, row_start(dev + 1) - first, per_row, 0)

        @pl.when(dev >= FIRST_W2)
        def _():
            first = w2_row_start(dev)

            def per_row(t, carry):
                row = first + t
                c = row // (FF // 16)
                kk = row % (FF // 16)
                for k in range(len(CHUNKS)):
                    n = CHUNKS[k]

                    @pl.when((kk >= 16 * OFFS[k]) & (kk < 16 * (OFFS[k] + n)))
                    def _():
                        base = 2 * (D // 8) * n + (kk - 16 * OFFS[k]) * ND

                        def per_col(j, carry2):
                            send(src2.at[pl.ds(t * 8, 8), j], k, c, base + j, send2.at[t])
                            return carry2

                        lax.fori_loop(0, ND, per_col, 0)
                return carry

            lax.fori_loop(0, w2_row_start(dev + 1) - first, per_row, 0)

        @pl.when(dev == 0)
        def _():
            for c in range(2):
                move(gain_src.at[0], out.at[0], send_gain.at[c], recv.at[0], c, GAIN_F, waiting)

    all_sends(False)
    all_sends(True)

    for k in range(len(CHUNKS)):
        part = out.at[pl.ds(SLOT0[k], TPD[k])]
        if k == 0:
            @pl.when(me_f != GAIN_F)
            def _():
                pltpu.make_async_copy(part, part, recv.at[k]).wait()

            @pl.when(me_f == GAIN_F)
            def _():
                pltpu.make_async_copy(out.at[0], out.at[0], recv.at[k]).wait()
        else:
            pltpu.make_async_copy(part, part, recv.at[k]).wait()


def spread_tiles(al13, al2, gain_tile):
    return pl.pallas_call(
        spread_kernel,
        out_shape=jax.ShapeDtypeStruct((SLOTS, 8, 1, 128), jnp.float32),
        in_specs=[pl.BlockSpec(memory_space=pltpu.VMEM)] * 3,
        out_specs=pl.BlockSpec(memory_space=pl.ANY),
        scratch_shapes=[
            pltpu.SemaphoreType.DMA((3,)),
            pltpu.SemaphoreType.DMA((15,)),
            pltpu.SemaphoreType.DMA((2,)),
            pltpu.SemaphoreType.DMA((3,)),
        ],
        compiler_params=pltpu.CompilerParams(has_side_effects=True),
        name='spread_tiles',
    )(al13, al2, gain_tile)


def return_kernel(g0, g1, g2, out13, out2, out_gain, send, send_gain, recv13, recv2, recv_gain):
    dev = my_index()
    me_c = lax.axis_index('dp')
    me_f = lax.axis_index('fsdp')

    def all_sends(waiting):
        def send_chunk(k, src):
            n = CHUNKS[k]

            def per_slot(s, carry):
                p = me_f * TPD[k] + s
                row13, col13, row2, col2 = tile_of(k, me_c, p)

                @pl.when(p < 2 * (D // 8) * n)
                def _():
                    owner = (8 * row13) // 21
                    t = row13 - row_start(owner)
                    move(src.at[s], out13.at[pl.ds(t * 8, 8), col13], send.at[k], recv13.at[t], owner // GRP, owner % GRP, waiting)

                @pl.when(p >= 2 * (D // 8) * n)
                def _():
                    owner = FIRST_W2 + (8 * row2 + 38) // 114
                    t = row2 - w2_row_start(owner)
                    move(src.at[s], out2.at[pl.ds(t * 8, 8), col2], send.at[k], recv2.at[t], owner // GRP, owner % GRP, waiting)
                return carry

            lax.fori_loop(0, TPD[k], per_slot, 0)

        send_chunk(2, g2)
        send_chunk(1, g1)

        @pl.when(me_f != GAIN_F)
        def _():
            send_chunk(0, g0)

        @pl.when(me_f == GAIN_F)
        def _():
            move(g0.at[0], out_gain.at[me_c], send_gain, recv_gain.at[me_c], 0, 0, waiting)

    all_sends(False)
    all_sends(True)

    @pl.when(dev < FIRST_W2)
    def _():
        def wait_row(t, carry):
            part = out13.at[pl.ds(t * 8, 8)]
            pltpu.make_async_copy(part, part, recv13.at[t]).wait()
            return carry

        lax.fori_loop(0, row_start(dev + 1) - row_start(dev), wait_row, 0)

    @pl.when(dev >= FIRST_W2)
    def _():
        def wait_row(t, carry):
            part = out2.at[pl.ds(t * 8, 8)]
            pltpu.make_async_copy(part, part, recv2.at[t]).wait()
            return carry

        lax.fori_loop(0, w2_row_start(dev + 1) - w2_row_start(dev), wait_row, 0)

    @pl.when(dev == 0)
    def _():
        for c in range(2):
            pltpu.make_async_copy(out_gain.at[c], out_gain.at[c], recv_gain.at[c]).wait()


def return_tiles(grads):
    tiles = [g.reshape(TPD[k], 8, 1, 128) for k, g in enumerate(grads)]
    return pl.pallas_call(
        return_kernel,
        out_shape=(
            jax.ShapeDtypeStruct((ROWS13, NB, 1, 128), jnp.float32),
            jax.ShapeDtypeStruct((ROWS2, ND, 1, 128), jnp.float32),
            jax.ShapeDtypeStruct((2, 8, 1, 128), jnp.float32),
        ),
        in_specs=[pl.BlockSpec(memory_space=pltpu.VMEM)] * 3,
        out_specs=[pl.BlockSpec(memory_space=pl.ANY)] * 3,
        scratch_shapes=[
            pltpu.SemaphoreType.DMA((3,)),
            pltpu.SemaphoreType.DMA,
            pltpu.SemaphoreType.DMA((3,)),
            pltpu.SemaphoreType.DMA((15,)),
            pltpu.SemaphoreType.DMA((2,)),
        ],
        compiler_params=pltpu.CompilerParams(has_side_effects=True),
        name='return_tiles',
    )(*tiles)


def region_offset(dev):
    first13 = D + 8 * FF * row_start(dev)
    first2 = W2_START + 8 * D * w2_row_start(dev)
    return jnp.where(dev <= FIRST_W2, first13, first2) - SHARD * dev


def chunk_weights(k, tiles):
    n = CHUNKS[k]
    part = (D // 8) * n
    w_one = tiles[:part].reshape(D // 8, n, 8, 128).transpose(0, 2, 1, 3).reshape(D, n * 128)
    w_three = tiles[part:2 * part].reshape(D // 8, n, 8, 128).transpose(0, 2, 1, 3).reshape(D, n * 128)
    w_two = tiles[2 * part:3 * part].reshape(16 * n, ND, 8, 128).transpose(0, 2, 1, 3).reshape(n * 128, D)
    return w_one, w_three, w_two


def chunk_tiles(k, d_one, d_three, d_two, tail):
    n = CHUNKS[k]
    t_one = d_one.reshape(D // 8, 8, n, 128).transpose(0, 2, 1, 3).reshape(-1, 8, 128)
    t_three = d_three.reshape(D // 8, 8, n, 128).transpose(0, 2, 1, 3).reshape(-1, 8, 128)
    t_two = d_two.reshape(16 * n, 8, ND, 128).transpose(0, 2, 1, 3).reshape(-1, 8, 128)
    parts = [t_one, t_three, t_two]
    if tail is not None:
        parts.append(tail)
    return jnp.concatenate(parts, axis=0)


def adam_update(master, adam_m, adam_v, grad_mean):
    m_new = BETA_ONE * adam_m + (1.0 - BETA_ONE) * grad_mean
    v_new = BETA_TWO * adam_v + (1.0 - BETA_TWO) * grad_mean * grad_mean
    m_hat = m_new / (1.0 - BETA_ONE ** ADAM_STEP)
    v_hat = v_new / (1.0 - BETA_TWO ** ADAM_STEP)
    master_new = master - LEARN_RATE * (m_hat / (jnp.sqrt(v_hat) + ADAM_EPS) + DECAY_RATE * master)
    return master_new, m_new, v_new


def dotf(a, b, dims):
    return lax.dot_general(a, b, (dims, ((), ())), preferred_element_type=jnp.float32)


def gather_weights(own):
    dev = my_index()
    ring = [(i, (i - 1) % NDEV) for i in range(NDEV)]
    spill = lax.ppermute(own[:SPILL], ('dp', 'fsdp'), ring)
    start = region_offset(dev)
    longer = jnp.concatenate([own, spill, jnp.zeros((SPILL + AL_LEN - SHARD - SPILL,), jnp.float32)])
    aligned = lax.dynamic_slice(longer, (start,), (AL_LEN,))
    al13 = aligned.reshape(ROWS13, NB, 1, 128)
    al2 = aligned[:ROWS2 * D].reshape(ROWS2, ND, 1, 128)
    gain_tile = own[:1024].reshape(1, 8, 1, 128)
    mine = spread_tiles(al13, al2, gain_tile).reshape(SLOTS, 8, 128).astype(jnp.bfloat16)
    gathered = []
    for k in range(len(CHUNKS)):
        part = mine[SLOT0[k]:SLOT0[k] + TPD[k]].reshape(TPD[k] * 8, 128)
        gathered.append(lax.all_gather(part, 'fsdp', axis=0, tiled=True).reshape(GRP * TPD[k], 8, 128))
    return gathered


def solution(mesh):
    flat_spec = P(None, ('dp', 'fsdp'))
    act_spec = P(None, ('dp', 'fsdp'), None, None)
    swap = [(0, 1), (1, 0)]

    def train_step(master, adam_m, adam_v, inputs, targets):
        token_total = inputs.shape[1] * inputs.shape[2]

        def local_step(master_sh, m_sh, v_sh, x_loc, y_loc):
            dev = my_index()
            tok = x_loc.shape[1] * x_loc.shape[2]
            own = master_sh.reshape(SHARD)
            x_own = x_loc.reshape(tok, D)
            y_own = y_loc.reshape(tok, D)
            gathered = gather_weights(own)
            x_all = jnp.concatenate([x_own, lax.ppermute(x_own, 'dp', swap)], axis=0)
            hidden = x_all.astype(jnp.float32)
            gain_f = gathered[0][GAIN_F * TPD[0]].reshape(1024)[:D].astype(jnp.float32)
            inv_rms = lax.rsqrt(jnp.mean(hidden * hidden, axis=-1, keepdims=True) + RMS_EPS)
            normed_f = hidden * inv_rms
            normed = (normed_f * gain_f).astype(jnp.bfloat16)

            saved = []
            h_part = None
            for k in range(len(CHUNKS)):
                w_one, w_three, w_two = chunk_weights(k, gathered[k])
                gate = dotf(normed, w_one, ((1,), (0,)))
                up = dotf(normed, w_three, ((1,), (0,)))
                inner = (jax.nn.silu(gate) * up).astype(jnp.bfloat16)
                piece = dotf(inner, w_two, ((1,), (0,)))
                h_part = piece if h_part is None else h_part + piece
                saved.append((gate, up, inner, w_one, w_three, w_two))

            other = lax.ppermute(h_part[tok:], 'dp', swap)
            hidden_out = hidden[:tok] + (h_part[:tok] + other)
            err = hidden_out - y_own.astype(jnp.float32)
            loss_sum = 0.5 * jnp.sum(err * err)
            err_b = err.astype(jnp.bfloat16)
            err_all = jnp.concatenate([err_b, lax.ppermute(err_b, 'dp', swap)], axis=0)

            grads = [None] * len(CHUNKS)
            q_sum = None
            for k in reversed(range(len(CHUNKS))):
                gate, up, inner, w_one, w_three, w_two = saved[k]
                sig = jax.nn.sigmoid(gate)
                d_two = dotf(inner, err_all, ((0,), (0,)))
                d_inner = dotf(err_all, w_two, ((1,), (1,)))
                d_gate = (d_inner * up * sig * (1.0 + gate * (1.0 - sig))).astype(jnp.bfloat16)
                d_up = (d_inner * (gate * sig)).astype(jnp.bfloat16)
                d_one = dotf(normed, d_gate, ((0,), (0,)))
                d_three = dotf(normed, d_up, ((0,), (0,)))
                q_k = dotf(d_gate, w_one, ((1,), (1,))) + dotf(d_up, w_three, ((1,), (1,)))
                q_sum = q_k if q_sum is None else q_sum + q_k
                tail = None
                if k == 0:
                    d_gain = jnp.sum(q_sum * normed_f, axis=0)
                    tail = jnp.pad(d_gain, (0, 1024 * TPD[0] - D)).reshape(TPD[0], 8, 128)
                tiles = chunk_tiles(k, d_one, d_three, d_two, tail)
                grads[k] = lax.psum_scatter(tiles.reshape(-1, 128), 'fsdp', scatter_dimension=0, tiled=True)

            loss_value = lax.psum(loss_sum, ('dp', 'fsdp')) / token_total
            out13, out2, out_gain = return_tiles(grads)
            flat13 = out13.reshape(AL_LEN)
            flat2 = jnp.pad(out2.reshape(ROWS2 * D), (0, AL_LEN - ROWS2 * D))
            aligned = jnp.where(dev < FIRST_W2, flat13, flat2)
            start = region_offset(dev)
            longer = jnp.concatenate([jnp.zeros((SPILL,), jnp.float32), aligned, jnp.zeros((SPILL,), jnp.float32)])
            spill = lax.dynamic_slice(longer, (SPILL + SHARD - start,), (SPILL,))
            body = lax.dynamic_slice(longer, (SPILL - start,), (SHARD,))
            ring = [(i, (i + 1) % NDEV) for i in range(NDEV)]
            head = lax.ppermute(spill, ('dp', 'fsdp'), ring)
            gain_grad = (out_gain[0] + out_gain[1]).reshape(1024)
            head = jnp.where(dev == 0, jnp.pad(gain_grad, (0, SPILL - 1024)), head)
            grad_sum = jnp.where(jnp.arange(SHARD) < start, jnp.pad(head, (0, SHARD - SPILL)), body)
            grad_mean = grad_sum.reshape(1, SHARD) / token_total
            master_new, m_new, v_new = adam_update(master_sh, m_sh, v_sh, grad_mean)
            return master_new, m_new, v_new, loss_value

        return jax.shard_map(local_step, mesh=mesh, in_specs=(flat_spec, flat_spec, flat_spec, act_spec, act_spec), out_specs=(flat_spec, flat_spec, flat_spec, P()), check_vma=False)(master, adam_m, adam_v, inputs, targets)

    return train_step
```

time: 1450 us -> 1310 us (0.903)
  local copies, waits for them, and re-layouts: 552 us -> 24.9 us
  waiting for transfers between devices: 587 us -> 903 us
  Pallas kernels: 0 us -> 40.8 us
  matrix products: 151 us -> 190 us
    reduce_scatter x0 -> x3, waiting for transfers between devices: none -> 697 us  [local_step(): lax.psum_scatter(tiles.reshape(-1, 128), 'fsdp', scatter_dimension=0, til...]
    unnamed x5 -> x6, waiting for transfers between devices: 452 us -> 0.11 us
    reshape x6 -> x2, local copies, waits for them, and re-layouts: 313 us -> 1.29 us  [the longest x1 1.28 us: gather_weights(): gain_tile = own[:1024].reshape(1, 8, 1, 128)]
    unnamed x27 -> x85, local copies, waits for them, and re-layouts: 124 us -> 9.33 us
    all_gather x1 -> x3, waiting for transfers between devices: 134 us -> 185 us  [gather_weights(): lax.all_gather(part, 'fsdp', axis=0, tiled=True)]
    slice x2 -> x8, local copies, waits for them, and re-layouts: 59.4 us -> 10.7 us  [the longest x2 8.04 us: chunk_weights(): tiles[2 * part:3 * part].reshape(16 * n, ND, 8, 128).transpose(0, 2, 1, 3)]
    pallas_call x0 -> x2, Pallas kernels: none -> 40.8 us  [the longest x1 21.1 us: return_tiles(): pl.pallas_call(return_kernel, out_shape=(jax.ShapeDtypeStruct((ROWS13, NB...]
    dot_general x6 -> x27, matrix products: 151 us -> 190 us  [dotf(): lax.dot_general(a, b, (dims, ((), ())), preferred_element_type=jnp.float32)]
  transfers between devices with their start and end apart: 3 -> 11, of which waited for: 2 -> 11; matrix products, arithmetic and copies ran while one was open for 0% -> 7% of each run, Pallas kernels for 0% -> 0%
where the time goes in v1:
time: 1310 us; the launch traced here: 1300 us
  waiting for transfers between devices  903 us (69%)
  matrix products  190 us (15%)
  blocking collectives  65 us (5%)
  other arithmetic  49.2 us (4%)
  Pallas kernels  40.8 us (3%)
  local copies, waits for them, and re-layouts  24.9 us (2%)
  between operations  17.4 us (1%)
  starting transfers between devices  13.1 us (1%)
    reduce_scatter x3, waiting for transfers between devices, local_step(): lax.psum_scatter(tiles.reshape(-1, 128), 'fsdp', scatter_dimension=0, til...  697 us
    dot_general x27, matrix products, dotf(): lax.dot_general(a, b, (dims, ((), ())), preferred_element_type=jnp.float32)  190 us
    all_gather x3, waiting for transfers between devices, gather_weights(): lax.all_gather(part, 'fsdp', axis=0, tiled=True)  185 us
    psum x1, blocking collectives, local_step(): loss_value = lax.psum(loss_sum, ('dp', 'fsdp')) / token_total  65 us
    reshape x3, other arithmetic, local_step(): tiles.reshape(-1, 128)  27.4 us
  transfers between devices with their start and end apart: 11, of which 11 were waited for; matrix products, arithmetic and copies ran while one was open for 7% of the time, Pallas kernels for 0%

profile of v1, /device:TPU:1, one launch (start us, length us, event | category | flops | bytes accessed | tf_op | source)
XLA Modules:
  0.0 1303.0 jit_solution(14238125883287059923)
XLA Ops:
  7.2 0.9 slice.83
  8.1 9.9 collective-permute-start.1
  18.0 2.1 reduce
  20.1 1.3 slice_bitcast_fusion.gain_src
  21.5 2.5 concatenate.22
  24.0 1.0 dynamic-slice
  25.0 1.0 dynamic_slice.9
  25.9 19.7 %spread_tiles.1 = f32[100,8,1,128]{3,2,1,0:T(1,128)} custom-call(f32[24,38,1,128]{3,2,1,0:T(1,128)} %bitcast.197, f32[120,7,1,128]{3,2,1,0:T(1,128)} %bitcast.210, f32[1,8,1,128]{3,2,1,0:T(1,128)} %slice_bitcast_fusion.gain_src), custom_call_target="tpu_custom_call" | custom-call | tf_op jit(solution)/shard_map/spread_tiles/pallas_call | solution.py:160
  45.6 1.3 convert_element_type.65
  49.8 3.6 collective-permute-done
  53.4 1.3 copy-done.6
  55.5 66.7 %all-gather.4.cloned.1.call-done = bf16[8192,128]{1,0:T(8,128)(2,1)} async-done(((bf16[128,128]{1,0:T(8,128)(2,1)}), bf16[8192,128]{1,0:T(8,128)(2,1)}) %all-gather.4.cloned.1.call-update) | async-done | bytes 2097168 | tf_op jit(solution)/shard_map/all_gather | solution.py:318
  122.9 3.1 multiply_convert_fusion.6
  126.2 2.2 fusion.19
  128.4 1.6 copy-done.29
  130.1 4.9 multiply_convert_fusion.9
  134.9 59.2 %all-gather.6.cloned.1.call-done = bf16[21504,128]{1,0:T(8,128)(2,1)} async-done(((bf16[336,128]{1,0:T(8,128)(2,1)}), bf16[21504,128]{1,0:T(8,128)(2,1)}) %all-gather.6.cloned.1.call-update) | async-done | bytes 5505040 | tf_op jit(solution)/shard_map/all_gather | solution.py:318
  194.1 4.9 fusion.15
  199.0 1.2 copy-done.15
  200.3 6.7 fusion.20
  206.9 59.0 %all-gather.8.cloned.1.call-done = bf16[21504,128]{1,0:T(8,128)(2,1)} async-done(((bf16[336,128]{1,0:T(8,128)(2,1)}), bf16[21504,128]{1,0:T(8,128)(2,1)}) %all-gather.8.cloned.1.call-update) | async-done | bytes 5505040 | tf_op jit(solution)/shard_map/all_gather | solution.py:318
  265.9 3.1 fusion.16
  269.6 6.8 fusion.22
  276.4 1.2 slice-done.3
  277.6 7.9 multiply_convert_fusion.5
  285.6 8.9 fusion.21
  294.5 7.9 multiply_convert_fusion.4
  302.5 8.8 fusion.23
  311.3 5.8 add_add_fusion
  317.4 2.3 collective-permute-start.2
  319.7 3.4 fusion.7
  323.0 2.7 collective-permute-done.2
  325.7 5.0 multiply_reduce_fusion.2
  331.1 3.5 collective-permute-done.3
  334.5 7.7 multiply_convert_fusion.7
  342.2 5.1 fusion.30
  347.4 2.1 fusion.24
  349.4 14.1 %multiply_convert_fusion.2 = (bf16[2048,1024]{1,0:T(8,128)(2,1)}, bf16[2048,1024]{1,0:T(8,128)(2,1)}) fusion(f32[2048,1024]{1,0:T(8,128)} %fusion.22, f32[2048,1024]{1,0:T(8,128)} %get-tuple-element.35, bf16[1024,896]{1,0:T(8,128)(2,1)} %bitcast.209, bf16[1024,896]{1,0:T(8,128)(2,1)} %copy-done.28, bf16[1024,896]{1,0:T(8,128)(2,1)S(1)} %get-tuple-element.11), kind=kOutput, calls=%fused_computation.4 | convolution fusion | flops 3792699392 | bytes 30670848 | tf_op jit(solution)/shard_map/dot_general | solution.py:301
  363.6 10.4 fusion.27
  373.9 6.6 fusion.26
  380.6 13.9 %multiply_convert_fusion = (bf16[2048,1024]{1,0:T(8,128)(2,1)}, bf16[2048,1024]{1,0:T(8,128)(2,1)}) fusion(f32[2048,1024]{1,0:T(8,128)} %fusion.20, f32[2048,1024]{1,0:T(8,128)} %get-tuple-element.37, bf16[1024,896]{1,0:T(8,128)(2,1)} %bitcast.202, bf16[1024,896]{1,0:T(8,128)(2,1)} %copy-done.28, bf16[1024,896]{1,0:T(8,128)(2,1)S(1)} %get-tuple-element.11), kind=kOutput, calls=%fused_computation.2 | convolution fusion | flops 3792699392 | bytes 30670848 | tf_op jit(solution)/shard_map/dot_general | solution.py:301
  394.5 10.4 fusion.29
  404.9 6.6 fusion.28
  411.5 3.2 fusion.25
  414.7 14.6 %multiply_reduce_fusion = f32[896]{0:T(1024)S(1)} fusion(f32[2048,896]{1,0:T(8,128)} %fusion.30, f32[2048,896]{1,0:T(8,128)} %fusion.28, f32[2048,896]{1,0:T(8,128)} %fusion.29, f32[2048,896]{1,0:T(8,128)} %fusion.26, f32[2048,896]{1,0:T(8,128)} %fusion.27, bf16[2048,384]{1,0:T(8,128)(2,1)S(1)} %get-tuple-element.19, bf16[896,384]{1,0:T(8,128)(2,1)} %bitcast.196, ...), kind=kOutput, calls=%fused_computation.12 | convolution fusion | flops 1431305344 | bytes 42642944 | tf_op jit(solution)/shard_map/dot_general | solution.py:301
  429.3 4.4 fusion.12
  433.7 2.3 maximum_bitcast_fusion.2
  436.1 1.4 copy-done.14
  437.5 7.2 fusion.8
  444.7 4.0 fusion.33
  448.7 4.1 fusion.34
  452.8 12.6 maximum_bitcast_fusion.1
  465.5 7.5 fusion.9
  473.0 4.0 fusion.31
  477.0 4.1 fusion.32
  481.1 12.5 maximum_bitcast_fusion
  494.5 65.0 %psum.7 = f32[]{:T(128)} all-reduce(f32[]{:T(128)S(6)} %mul_shard_map.3), channel_id=1, replica_groups=mesh['dp'=2,'fsdp'=64] {'dp','fsdp'}, use_global_device_ids=true, to_apply=%region_6.7 | all-reduce | flops 1 | bytes 8 | tf_op jit(solution)/shard_map/psum | solution.py:382
  560.2 186.9 %reduce-scatter.4.cloned.1.call-done = f32[128,128]{1,0:T(8,128)} async-done(((f32[8192,128]{1,0:T(8,128)}), f32[128,128]{1,0:T(8,128)}) %reduce-scatter.4.cloned.1.call-update) | async-done | bytes 65552 | tf_op jit(solution)/shard_map/reduce_scatter | solution.py:380
  747.1 277.0 %reduce-scatter.8.cloned.1.call-done = f32[336,128]{1,0:T(8,128)} async-done(((f32[21504,128]{1,0:T(8,128)}), f32[336,128]{1,0:T(8,128)}) %reduce-scatter.8.cloned.1.call-update) | async-done | bytes 172048 | tf_op jit(solution)/shard_map/reduce_scatter | solution.py:380
  1024.1 233.2 %reduce-scatter.6.cloned.1.call-done = f32[336,128]{1,0:T(8,128)} async-done(((f32[21504,128]{1,0:T(8,128)}), f32[336,128]{1,0:T(8,128)}) %reduce-scatter.6.cloned.1.call-update) | async-done | bytes 172048 | tf_op jit(solution)/shard_map/reduce_scatter | solution.py:380
  1257.4 21.1 %return_tiles.1 = (f32[24,38,1,128]{3,2,1,0:T(1,128)}, f32[120,7,1,128]{3,2,1,0:T(1,128)}, f32[2,8,1,128]{3,2,1,0:T(1,128)}) custom-call(f32[16,8,1,128]{3,2,1,0:T(1,128)} %bitcast.220, f32[42,8,1,128]{3,2,1,0:T(1,128)} %bitcast.217, f32[42,8,1,128]{3,2,1,0:T(1,128)} %bitcast.216), custom_call_target="tpu_custom_call" | custom-call | tf_op jit(solution)/shard_map/return_tiles/pallas_call | solution.py:244
  1278.5 1.2 pad_select_fusion
  1280.6 10.7 collective-permute-done.4
  1291.6 3.3 multiply_subtract_fusion
  (113 shorter events, 7.1 us)
Async XLA Ops:
  7.2 115.0 %all-gather.4.cloned.1.call-start = ((), (), s32[]{:S(2)}) async-start(), calls=%async_computation.3 | async-start | bytes 2129920 | tf_op jit(solution)/shard_map/all_gather | solution.py:318
  8.1 13.4 %collective-permute-start.1 = (f32[35840]{0:T(1024)S(1)}, f32[35840]{0:T(1024)S(1)}, u32[]{:S(2)}, u32[]{:S(2)}) collective-permute-start(f32[35840]{0:T(1024)S(1)} %bitcast.218), channel_id=1, source_target_pairs={{0,127},{1,0},{2,1},{3,2},{4,3},{5,4},{6,5},{7,6},{8,7},{9,8},{10,... | collective-permute-start | bytes 430088 | tf_op jit(solution)/shard_map/ppermute | solution.py:307
  18.0 31.5 %copy-start.5 = (bf16[1,4,256,896]{3,2,1,0:T(8,128)(2,1)S(1)}, bf16[1,4,256,896]{3,2,1,0:T(8,128)(2,1)}, u32[]{:S(2)}) copy-start(bf16[1,4,256,896]{3,2,1,0:T(8,128)(2,1)} %param.8) | copy-start | bytes 5505028
  47.7 146.5 %all-gather.6.cloned.1.call-start = ((), (), s32[]{:S(2)}) async-start(), calls=%async_computation.4 | async-start | bytes 5591040 | tf_op jit(solution)/shard_map/all_gather | solution.py:318
  48.7 217.2 %all-gather.8.cloned.1.call-start = ((), (), s32[]{:S(2)}) async-start(), calls=%async_computation.5 | async-start | bytes 5591040 | tf_op jit(solution)/shard_map/all_gather | solution.py:318
  49.5 697.6 %reduce-scatter.4.cloned.1.call-start = ((), (), s32[]{:S(2)}) async-start(), calls=%async_computation.6 | async-start | bytes 4259840 | tf_op jit(solution)/shard_map/reduce_scatter | solution.py:380
  49.5 3.9 collective-permute-start
  53.4 1.3 copy-start.6
  55.5 67.4 %copy-start.26 = (f32[2048]{0:T(1024)}, f32[2048]{0:T(1024)S(1)}, u32[]{:S(2)}) copy-start(f32[2048]{0:T(1024)S(1)} %add_rsqrt_fusion) | copy-start | bytes 24580
  122.9 3.1 copy-start.11
  126.0 2.4 copy-start
  126.2 2.3 copy-start.9
  128.4 1.7 copy-start.29
  194.1 6.2 copy-start.1
  199.0 1.2 copy-start.15
  265.9 3.7 copy-start.2
  265.9 10.5 slice-start.2
  269.1 7.4 copy-start.19
  269.1 25.4 %copy-start.21 = (bf16[7168,128]{1,0:T(8,128)(2,1)}, bf16[7168,128]{1,0:T(8,128)(2,1)S(1)}, u32[]{:S(2)}) copy-start(bf16[7168,128]{1,0:T(8,128)(2,1)S(1)} %get-tuple-element.25) | copy-start | bytes 5505028
  269.1 33.4 %copy-start.22 = (bf16[7168,128]{1,0:T(8,128)(2,1)}, bf16[7168,128]{1,0:T(8,128)(2,1)S(1)}, u32[]{:S(2)}) copy-start(bf16[7168,128]{1,0:T(8,128)(2,1)S(1)} %get-tuple-element.24) | copy-start | bytes 5505028
  269.6 6.8 copy-start.17
  269.6 8.0 slice-start.3
  277.6 7.9 copy-start.18
  285.6 9.0 copy-start.36
  302.5 8.8 slice-start
  302.5 8.8 slice-start.1
  302.5 8.8 copy-start.23
  317.1 2.6 copy-start.7
  317.4 8.4 copy-start.12
  317.4 8.3 collective-permute-start.2
  330.8 49.8 %copy-start.13 = (bf16[1024,896]{1,0:T(8,128)(2,1)}, bf16[1024,896]{1,0:T(8,128)(2,1)S(1)}, u32[]{:S(2)}) copy-start(bf16[1024,896]{1,0:T(8,128)(2,1)S(1)} %get-tuple-element.11) | copy-start | bytes 5505028
  330.8 3.8 collective-permute-start.3
  334.5 7.7 copy-start.28
  363.5 10.4 copy-start.20
  363.5 10.4 copy-start.34
  394.5 10.4 copy-start.16
  394.5 10.4 copy-start.31
  411.5 3.2 copy-start.27
  429.2 4.4 copy-start.8
  436.0 1.5 copy-start.14
  436.0 588.1 %reduce-scatter.8.cloned.1.call-start = ((), (), s32[]{:S(2)}) async-start(), calls=%async_computation.8 | async-start | bytes 11182080 | tf_op jit(solution)/shard_map/reduce_scatter | solution.py:380
  437.5 7.2 copy-start.3
  437.5 7.2 copy-start.35
  444.7 4.0 copy-start.33
  465.4 791.9 %reduce-scatter.6.cloned.1.call-start = ((), (), s32[]{:S(2)}) async-start(), calls=%async_computation.7 | async-start | bytes 11182080 | tf_op jit(solution)/shard_map/reduce_scatter | solution.py:380
  465.5 7.5 copy-start.4
  465.5 7.5 copy-start.32
  473.0 4.0 copy-start.30
  493.7 797.9 %copy-start.10 = (f32[1,102151]{1,0:T(1,128)S(1)}, f32[1,102151]{1,0:T(1,128)}, u32[]{:S(2)}) copy-start(f32[1,102151]{1,0:T(1,128)} %param.5) | copy-start | bytes 1225816
  493.7 797.9 %copy-start.24 = (f32[1,102151]{1,0:T(1,128)S(1)}, f32[1,102151]{1,0:T(1,128)}, u32[]{:S(2)}) copy-start(f32[1,102151]{1,0:T(1,128)} %param.6) | copy-start | bytes 1225816
  493.7 797.9 %copy-start.25 = (f32[1,102151]{1,0:T(1,128)S(1)}, f32[1,102151]{1,0:T(1,128)}, u32[]{:S(2)}) copy-start(f32[1,102151]{1,0:T(1,128)} %param.7) | copy-start | bytes 1225816
  1279.9 11.5 collective-permute-start.4
Sparse Core Ops, SparseCore 0:
  47.8 74.3 all-gather.3
  125.5 68.5 all-gather.5
  197.4 68.4 all-gather.7
  436.1 310.9 reduce-scatter.3
  751.6 272.5 reduce-scatter.7
  1028.6 228.6 reduce-scatter.5

commit v2 on v1

v2 whole, which is shorter than its diff:
```python
import functools

import jax
import jax.numpy as jnp
from jax import lax
from jax.experimental import pallas as pl
from jax.experimental.pallas import tpu as pltpu
from jax.sharding import PartitionSpec as P

ADAM_STEP = 3
LEARN_RATE = 2e-3
BETA_ONE = 0.9
BETA_TWO = 0.999
ADAM_EPS = 1e-8
DECAY_RATE = 0.1
RMS_EPS = 1e-5

D = 896
FF = 4864
FLAT = D * (3 * FF + 1)
NDEV = 128
GRP = 64
SHARD = FLAT // NDEV
NB = FF // 128
ND = D // 128
HB = NB // 2
W2_START = D + 2 * D * FF
FIRST_W2 = 85
SPILL = 35840
ROWS13, ROWS2 = 24, 120
AL_LEN = ROWS13 * FF

MAT = (D // 8) * HB
SLOTS = 100
GAIN_F = GRP - 1
GAIN_SLOT = 3 * MAT - GAIN_F * SLOTS
ROWS = SLOTS * 8
COLOURS = (((0, 144), (144, 128)), ((272, 144), (416, 128)), ((544, 128), (672, 128)))
SUMS = (((0, 17), (17, 17)), ((34, 17), (51, 16)), ((67, 17), (84, 16)))
AXES = ('z', 'y', 'x')

MESH = pl.DeviceIdType.MESH


def row_start(dev):
    return (21 * dev + 7) // 8


def w2_row_start(dev):
    return jnp.maximum((114 * dev - 9728 + 7) // 8, 0)


def my_index():
    return lax.axis_index('dp') * GRP + lax.axis_index('fsdp')


def move(src, dst, send_sem, recv_sem, c, f, waiting):
    stays = (c == lax.axis_index('dp')) & (f == lax.axis_index('fsdp'))

    def remote():
        return pltpu.make_async_remote_copy(
            src_ref=src, dst_ref=dst, send_sem=send_sem, recv_sem=recv_sem, device_id=(c, f), device_id_type=MESH)

    if waiting:
        @pl.when(jnp.logical_not(stays))
        def _():
            remote().wait_send()
    else:
        @pl.when(jnp.logical_not(stays))
        def _():
            remote().start()

        @pl.when(stays)
        def _():
            pltpu.make_async_copy(src, dst, recv_sem).start()


def ring_pos():
    f = lax.axis_index('fsdp')
    return {'z': f // 16, 'y': (f // 4) % 4, 'x': f % 4}


def neighbour(pos, axis, step):
    moved = dict(pos)
    moved[axis] = (pos[axis] + step + 4) % 4
    return (lax.axis_index('dp'), moved['z'] * 16 + moved['y'] * 4 + moved['x'])


def block_set(pos, fixed, rows):
    index = tuple(fixed.get(axis, slice(None)) for axis in AXES)
    return index + (pl.ds(rows[0], rows[1]), slice(None))


def gather_kernel(src13, src2, gain_src, out, land, mine, send13, send2, send_gain, recv_tile, local_sem, send_sem, recv_sem):
    dev = my_index()
    me_f = lax.axis_index('fsdp')
    pos = ring_pos()

    def all_sends(waiting):
        def send(src, c, p, sem):
            move(src, land.at[p % SLOTS], sem, recv_tile, c, p // SLOTS, waiting)

        @pl.when(dev < FIRST_W2)
        def _():
            first = row_start(dev)

            def per_row(t, carry):
                def per_col(j, carry2):
                    for c in range(2):
                        send(src13.at[pl.ds(t * 8, 8), HB * c + j, 0], c, (first + t) * HB + j, send13.at[t])
                    return carry2

                return lax.fori_loop(0, HB, per_col, carry)

            lax.fori_loop(0, row_start(dev + 1) - first, per_row, 0)

        @pl.when(dev >= FIRST_W2)
        def _():
            first = w2_row_start(dev)

            def per_row(t, carry):
                row = first + t
                c = row // (FF // 16)
                base = 2 * MAT + (row % (FF // 16)) * ND

                def per_col(j, carry2):
                    send(src2.at[pl.ds(t * 8, 8), j, 0], c, base + j, send2.at[t])
                    return carry2

                return lax.fori_loop(0, ND, per_col, carry)

            lax.fori_loop(0, w2_row_start(dev + 1) - first, per_row, 0)

        @pl.when(dev == 0)
        def _():
            for c in range(2):
                move(gain_src.at[0, pl.ds(0, 8), 0], land.at[GAIN_SLOT], send_gain.at[c], recv_tile, c, GAIN_F, waiting)

    all_sends(False)
    all_sends(True)

    @pl.when(me_f != GAIN_F)
    def _():
        pltpu.make_async_copy(land, land, recv_tile).wait()

    @pl.when(me_f == GAIN_F)
    def _():
        part = land.at[pl.ds(0, GAIN_SLOT + 1)]
        pltpu.make_async_copy(part, part, recv_tile).wait()

    mine[...] = land[...].reshape(ROWS, 128).astype(jnp.bfloat16)
    own = out.at[pos['z'], pos['y'], pos['x']]
    local = pltpu.make_async_copy(mine, own, local_sem)
    local.start()
    local.wait()

    for phase in range(3):
        def copies(colour, step):
            axis = AXES[(2 - colour - phase) % 3]
            done = [AXES[(2 - colour - q) % 3] for q in range(phase)]
            fixed = {a: pos[a] for a in AXES if a not in done}
            halves = COLOURS[colour]
            both = (halves[0][0], halves[0][1] + halves[1][1])
            made = []
            for way, shift in enumerate((1, -1)):
                where = dict(fixed)
                rows = both
                if step == 1:
                    where[axis] = (pos[axis] - shift + 4) % 4
                    rows = halves[way]
                index = block_set(pos, where, rows)
                made.append(pltpu.make_async_remote_copy(
                    src_ref=out.at[index],
                    dst_ref=out.at[index],
                    send_sem=send_sem.at[colour, phase, step, way],
                    recv_sem=recv_sem.at[colour, phase, step, way],
                    device_id=neighbour(pos, axis, shift),
                    device_id_type=MESH,
                ))
            return made

        for step in range(2):
            for colour in range(3):
                for copy in copies(colour, step):
                    copy.start()
            for colour in range(3):
                for copy in copies(colour, step):
                    copy.wait()


def gather_tiles(al13, al2, gain_tile):
    return pl.pallas_call(
        gather_kernel,
        out_shape=jax.ShapeDtypeStruct((4, 4, 4, ROWS, 128), jnp.bfloat16),
        in_specs=[pl.BlockSpec(memory_space=pltpu.VMEM)] * 3,
        out_specs=pl.BlockSpec(memory_space=pl.ANY),
        scratch_shapes=[
            pltpu.VMEM((SLOTS, 8, 128), jnp.float32),
            pltpu.VMEM((ROWS, 128), jnp.bfloat16),
            pltpu.SemaphoreType.DMA((3,)),
            pltpu.SemaphoreType.DMA((15,)),
            pltpu.SemaphoreType.DMA((2,)),
            pltpu.SemaphoreType.DMA,
            pltpu.SemaphoreType.DMA,
            pltpu.SemaphoreType.DMA((3, 3, 2, 2)),
            pltpu.SemaphoreType.DMA((3, 3, 2, 2)),
        ],
        compiler_params=pltpu.CompilerParams(has_side_effects=True),
        name='gather_tiles',
    )(al13, al2, gain_tile)


def scatter_kernel(g_one, g_three, g_two, g_tail, out13, out2, out_gain, total, relay0, relay1, relay2, merge0, merge1, merge2,
                   load_sem, send_sem, recv_sem, send_tile, send_gain, recv13, recv2, recv_gain):
    dev = my_index()
    me_c = lax.axis_index('dp')
    me_f = lax.axis_index('fsdp')
    pos = ring_pos()
    relays = (relay0, relay1, relay2)
    merges = (merge0, merge1, merge2)

    sources = ((g_one, 0, MAT), (g_three, MAT, 2 * MAT), (g_two, 2 * MAT, 3 * MAT), (g_tail, 3 * MAT, GRP * SLOTS))
    loads = []
    for f in range(GRP):
        for src, low, high in sources:
            first, last = max(low, f * SLOTS), min(high, (f + 1) * SLOTS)
            if first < last:
                dst = total.at[f // 16, (f // 4) % 4, f % 4, pl.ds(first - f * SLOTS, last - first)]
                loads.append(pltpu.make_async_copy(src.at[pl.ds(first - low, last - first)], dst, load_sem.at[len(loads)]))
    for copy in loads:
        copy.start()
    for copy in loads:
        copy.wait()

    for phase in range(3):
        def index_of(colour, at, rows):
            axis = AXES[(colour + phase) % 3]
            done = [AXES[(colour + q) % 3] for q in range(phase)]
            fixed = {a: pos[a] for a in done}
            fixed[axis] = at
            return fixed, rows

        def set_ref(colour, at, rows):
            fixed, rows = index_of(colour, at, rows)
            return total.at[tuple(fixed.get(a, slice(None)) for a in AXES) + (pl.ds(rows[0], rows[1]),)]

        def add_set(colour, at, rows, landed):
            fixed, rows = index_of(colour, at, rows)
            free = [a for a in AXES if a not in fixed]

            def body(i, carry):
                spot = dict(fixed)
                inner = ()
                if len(free) == 2:
                    inner = (i // 4, i % 4)
                elif len(free) == 1:
                    inner = (i,)
                for a, v in zip(free, inner):
                    spot[a] = v
                where = (spot['z'], spot['y'], spot['x'], pl.ds(rows[0], rows[1]))
                value = total[where]
                for part in landed:
                    value = value + part[inner + (pl.ds(0, rows[1]),)]
                total[where] = value
                return carry

            lax.fori_loop(0, 4 ** len(free), body, 0)

        def position(colour):
            return pos[AXES[(colour + phase) % 3]]

        def both(colour):
            halves = SUMS[colour]
            return (halves[0][0], halves[0][1] + halves[1][1])

        def copies(colour, step):
            axis = AXES[(colour + phase) % 3]
            made = []
            for way, shift in enumerate((1, -1)):
                if step == 0:
                    rows = SUMS[colour][way]
                    at = (pos[axis] + 2) % 4
                    dst = relays[phase]
                else:
                    rows = both(colour)
                    at = (pos[axis] + shift + 4) % 4
                    dst = merges[phase]
                lead = (colour, way) + (slice(None),) * (2 - phase)
                made.append(pltpu.make_async_remote_copy(
                    src_ref=set_ref(colour, at, rows),
                    dst_ref=dst.at[lead + (pl.ds(0, rows[1]),)],
                    send_sem=send_sem.at[colour, phase, step, way],
                    recv_sem=recv_sem.at[colour, phase, step, way],
                    device_id=neighbour(pos, axis, shift),
                    device_id_type=MESH,
                ))
            return made

        for colour in range(3):
            for copy in copies(colour, 0):
                copy.start()
        for colour in range(3):
            for copy in copies(colour, 0):
                copy.wait()
            here = position(colour)
            add_set(colour, (here + 1) % 4, SUMS[colour][0], [relays[phase].at[colour, 0]])
            add_set(colour, (here + 3) % 4, SUMS[colour][1], [relays[phase].at[colour, 1]])
            for copy in copies(colour, 1):
                copy.start()
        for colour in range(3):
            for copy in copies(colour, 1):
                copy.wait()
            add_set(colour, position(colour), both(colour), [merges[phase].at[colour, 0], merges[phase].at[colour, 1]])

    mine = total.at[pos['z'], pos['y'], pos['x']]

    def all_sends(waiting):
        def per_slot(s, carry):
            p = me_f * SLOTS + s

            @pl.when(p < 2 * MAT)
            def _():
                row = p // HB
                owner = (8 * row) // 21
                t = row - row_start(owner)
                dst = out13.at[pl.ds(t * 8, 8), HB * me_c + p % HB, 0]
                move(mine.at[s], dst, send_tile, recv13.at[t], owner // GRP, owner % GRP, waiting)

            @pl.when(p >= 2 * MAT)
            def _():
                row = (FF // 16) * me_c + (p - 2 * MAT) // ND
                owner = FIRST_W2 + (8 * row + 38) // 114
                t = row - w2_row_start(owner)
                dst = out2.at[pl.ds(t * 8, 8), (p - 2 * MAT) % ND, 0]
                move(mine.at[s], dst, send_tile, recv2.at[t], owner // GRP, owner % GRP, waiting)
            return carry

        lax.fori_loop(0, jnp.where(me_f == GAIN_F, GAIN_SLOT, SLOTS), per_slot, 0)

        @pl.when(me_f == GAIN_F)
        def _():
            def per_device(d, carry):
                move(mine.at[GAIN_SLOT], out_gain.at[me_c], send_gain, recv_gain.at[me_c], d // GRP, d % GRP, waiting)
                return carry

            lax.fori_loop(0, NDEV, per_device, 0)

    all_sends(False)
    all_sends(True)

    @pl.when(dev < FIRST_W2)
    def _():
        def wait_row(t, carry):
            part = out13.at[pl.ds(t * 8, 8)]
            pltpu.make_async_copy(part, part, recv13.at[t]).wait()
            return carry

        lax.fori_loop(0, row_start(dev + 1) - row_start(dev), wait_row, 0)

    @pl.when(dev >= FIRST_W2)
    def _():
        def wait_row(t, carry):
            part = out2.at[pl.ds(t * 8, 8)]
            pltpu.make_async_copy(part, part, recv2.at[t]).wait()
            return carry

        lax.fori_loop(0, w2_row_start(dev + 1) - w2_row_start(dev), wait_row, 0)

    for c in range(2):
        pltpu.make_async_copy(out_gain.at[c], out_gain.at[c], recv_gain.at[c]).wait()


def scatter_tiles(g_one, g_three, g_two, g_tail):
    half = max(h[1] for pair in SUMS for h in pair)
    full = max(pair[0][1] + pair[1][1] for pair in SUMS)
    relays = [pltpu.VMEM((3, 2) + (4,) * (2 - p) + (half, 8, 128), jnp.float32) for p in range(3)]
    merges = [pltpu.VMEM((3, 2) + (4,) * (2 - p) + (full, 8, 128), jnp.float32) for p in range(3)]
    return pl.pallas_call(
        scatter_kernel,
        out_shape=(
            jax.ShapeDtypeStruct((ROWS13, NB, 1, 128), jnp.float32),
            jax.ShapeDtypeStruct((ROWS2, ND, 1, 128), jnp.float32),
            jax.ShapeDtypeStruct((2, 8, 128), jnp.float32),
        ),
        in_specs=[pl.BlockSpec(memory_space=pl.ANY)] * 4,
        out_specs=[pl.BlockSpec(memory_space=pl.ANY)] * 3,
        scratch_shapes=[
            pltpu.VMEM((4, 4, 4, SLOTS, 8, 128), jnp.float32),
            *relays,
            *merges,
            pltpu.SemaphoreType.DMA((GRP + 3,)),
            pltpu.SemaphoreType.DMA((3, 3, 2, 2)),
            pltpu.SemaphoreType.DMA((3, 3, 2, 2)),
            pltpu.SemaphoreType.DMA,
            pltpu.SemaphoreType.DMA,
            pltpu.SemaphoreType.DMA((3,)),
            pltpu.SemaphoreType.DMA((15,)),
            pltpu.SemaphoreType.DMA((2,)),
        ],
        compiler_params=pltpu.CompilerParams(has_side_effects=True, vmem_limit_bytes=60 * 2 ** 20),
        name='scatter_tiles',
    )(g_one, g_three, g_two, g_tail)


def region_offset(dev):
    first13 = D + 8 * FF * row_start(dev)
    first2 = W2_START + 8 * D * w2_row_start(dev)
    return jnp.where(dev <= FIRST_W2, first13, first2) - SHARD * dev


def as_matrix(tiles, rows, cols):
    return tiles.reshape(rows // 8, cols // 128, 8, 128).transpose(0, 2, 1, 3).reshape(rows, cols)


def as_tiles(matrix):
    rows, cols = matrix.shape
    return matrix.reshape(rows // 8, 8, cols // 128, 128).transpose(0, 2, 1, 3).reshape(-1, 8, 128)


def adam_update(master, adam_m, adam_v, grad_mean):
    m_new = BETA_ONE * adam_m + (1.0 - BETA_ONE) * grad_mean
    v_new = BETA_TWO * adam_v + (1.0 - BETA_TWO) * grad_mean * grad_mean
    m_hat = m_new / (1.0 - BETA_ONE ** ADAM_STEP)
    v_hat = v_new / (1.0 - BETA_TWO ** ADAM_STEP)
    master_new = master - LEARN_RATE * (m_hat / (jnp.sqrt(v_hat) + ADAM_EPS) + DECAY_RATE * master)
    return master_new, m_new, v_new


def dotf(a, b, dims):
    return lax.dot_general(a, b, (dims, ((), ())), preferred_element_type=jnp.float32)


def gather_weights(own):
    dev = my_index()
    ring = [(i, (i - 1) % NDEV) for i in range(NDEV)]
    spill = lax.ppermute(own[:SPILL], ('dp', 'fsdp'), ring)
    start = region_offset(dev)
    longer = jnp.concatenate([own, spill, jnp.zeros((SPILL + AL_LEN - SHARD - SPILL,), jnp.float32)])
    aligned = lax.dynamic_slice(longer, (start,), (AL_LEN,))
    al13 = aligned.reshape(ROWS13, NB, 1, 128)
    al2 = aligned[:ROWS2 * D].reshape(ROWS2, ND, 1, 128)
    gain_tile = own[:1024].reshape(1, 8, 1, 128)
    return gather_tiles(al13, al2, gain_tile).reshape(GRP * SLOTS, 8, 128)


def solution(mesh):
    flat_spec = P(None, ('dp', 'fsdp'))
    act_spec = P(None, ('dp', 'fsdp'), None, None)
    swap = [(0, 1), (1, 0)]

    def train_step(master, adam_m, adam_v, inputs, targets):
        token_total = inputs.shape[1] * inputs.shape[2]

        def local_step(master_sh, m_sh, v_sh, x_loc, y_loc):
            dev = my_index()
            tok = x_loc.shape[1] * x_loc.shape[2]
            own = master_sh.reshape(SHARD)
            x_own = x_loc.reshape(tok, D)
            y_own = y_loc.reshape(tok, D)
            tiles = gather_weights(own)
            w_one = as_matrix(tiles[:MAT], D, HB * 128)
            w_three = as_matrix(tiles[MAT:2 * MAT], D, HB * 128)
            w_two = as_matrix(tiles[2 * MAT:3 * MAT], HB * 128, D)
            gain_f = tiles[GAIN_F * SLOTS + GAIN_SLOT].reshape(1024)[:D].astype(jnp.float32)
            x_all = jnp.concatenate([x_own, lax.ppermute(x_own, 'dp', swap)], axis=0)
            hidden = x_all.astype(jnp.float32)
            inv_rms = lax.rsqrt(jnp.mean(hidden * hidden, axis=-1, keepdims=True) + RMS_EPS)
            normed_f = hidden * inv_rms
            normed = (normed_f * gain_f).astype(jnp.bfloat16)
            gate = dotf(normed, w_one, ((1,), (0,)))
            up = dotf(normed, w_three, ((1,), (0,)))
            inner = (jax.nn.silu(gate) * up).astype(jnp.bfloat16)
            h_part = dotf(inner, w_two, ((1,), (0,)))
            other = lax.ppermute(h_part[tok:], 'dp', swap)
            err = hidden[:tok] + (h_part[:tok] + other) - y_own.astype(jnp.float32)
            loss_sum = 0.5 * jnp.sum(err * err)
            err_b = err.astype(jnp.bfloat16)
            err_all = jnp.concatenate([err_b, lax.ppermute(err_b, 'dp', swap)], axis=0)

            sig = jax.nn.sigmoid(gate)
            d_two = dotf(inner, err_all, ((0,), (0,)))
            d_inner = dotf(err_all, w_two, ((1,), (1,)))
            d_gate = (d_inner * up * sig * (1.0 + gate * (1.0 - sig))).astype(jnp.bfloat16)
            d_up = (d_inner * (gate * sig)).astype(jnp.bfloat16)
            d_one = dotf(normed, d_gate, ((0,), (0,)))
            d_three = dotf(normed, d_up, ((0,), (0,)))
            q_sum = dotf(d_gate, w_one, ((1,), (1,))) + dotf(d_up, w_three, ((1,), (1,)))
            d_gain = jnp.sum(q_sum * normed_f, axis=0)
            tail = jnp.concatenate([d_gain, loss_sum.reshape(1)])
            tail = jnp.pad(tail, (0, 1024 * (SLOTS - GAIN_SLOT) - D - 1)).reshape(SLOTS - GAIN_SLOT, 8, 128)
            out13, out2, out_gain = scatter_tiles(as_tiles(d_one), as_tiles(d_three), as_tiles(d_two), tail)
            sums = (out_gain[0] + out_gain[1]).reshape(1024)
            loss_value = sums[D] / token_total
            flat13 = out13.reshape(AL_LEN)
            flat2 = jnp.pad(out2.reshape(ROWS2 * D), (0, AL_LEN - ROWS2 * D))
            aligned = jnp.where(dev < FIRST_W2, flat13, flat2)
            start = region_offset(dev)
            longer = jnp.concatenate([jnp.zeros((SPILL,), jnp.float32), aligned, jnp.zeros((SPILL,), jnp.float32)])
            spill = lax.dynamic_slice(longer, (SPILL + SHARD - start,), (SPILL,))
            body = lax.dynamic_slice(longer, (SPILL - start,), (SHARD,))
            ring = [(i, (i + 1) % NDEV) for i in range(NDEV)]
            head = lax.ppermute(spill, ('dp', 'fsdp'), ring)
            head = jnp.where(dev == 0, jnp.pad(sums[:D], (0, SPILL - D)), head)
            grad_sum = jnp.where(jnp.arange(SHARD) < start, jnp.pad(head, (0, SHARD - SPILL)), body)
            grad_mean = grad_sum.reshape(1, SHARD) / token_total
            master_new, m_new, v_new = adam_update(master_sh, m_sh, v_sh, grad_mean)
            return master_new, m_new, v_new, loss_value

        return jax.shard_map(local_step, mesh=mesh, in_specs=(flat_spec, flat_spec, flat_spec, act_spec, act_spec), out_specs=(flat_spec, flat_spec, flat_spec, P()), check_vma=False)(master, adam_m, adam_v, inputs, targets)

    return train_step
```

time: 1310 us -> 462 us (0.35)
  waiting for transfers between devices: 903 us -> 14.4 us
  Pallas kernels: 40.8 us -> 227 us
  blocking collectives: 65 us -> 0 us
  other arithmetic: 49.2 us -> 20.2 us
  matrix products: 190 us -> 161 us
  between operations: 17.4 us -> 3.5 us
    reduce_scatter x3 -> x0, waiting for transfers between devices: 697 us -> none  [local_step(): lax.psum_scatter(tiles.reshape(-1, 128), 'fsdp', scatter_dimension=0, til...]
    pallas_call x2, Pallas kernels: 40.8 us -> 227 us  [the longest x1 140 us: scatter_tiles(): pl.pallas_call(scatter_kernel, out_shape=(jax.ShapeDtypeStruct((ROWS13, N...]
    all_gather x3 -> x0, waiting for transfers between devices: 185 us -> none  [gather_weights(): lax.all_gather(part, 'fsdp', axis=0, tiled=True)]
    psum x1 -> x0, blocking collectives: 65 us -> none  [local_step(): loss_value = lax.psum(loss_sum, ('dp', 'fsdp')) / token_total]
    dot_general x27 -> x9, matrix products: 190 us -> 161 us  [dotf(): lax.dot_general(a, b, (dims, ((), ())), preferred_element_type=jnp.float32)]
    reshape x3 -> x1, other arithmetic: 27.4 us -> 0.64 us  [local_step(): jnp.pad(tail, (0, 1024 * (SLOTS - GAIN_SLOT) - D - 1))]
  transfers between devices with their start and end apart: 11 -> 5, of which waited for: 11 -> 3; matrix products, arithmetic and copies ran while one was open for 7% -> 4% of each run, Pallas kernels for 0% -> 19%
where the time goes in v2:
time: 462 us; the launch traced here: 459 us
  Pallas kernels  227 us (49%)
  matrix products  161 us (35%)
  other arithmetic  20.2 us (4%)
  starting transfers between devices  17.3 us (4%)
  local copies, waits for them, and re-layouts  15.2 us (3%)
  waiting for transfers between devices  14.4 us (3%)
    dot_general x9, matrix products, dotf(): lax.dot_general(a, b, (dims, ((), ())), preferred_element_type=jnp.float32)  161 us
    pallas_call x1, Pallas kernels, scatter_tiles(): pl.pallas_call(scatter_kernel, out_shape=(jax.ShapeDtypeStruct((ROWS13, N...  140 us
    pallas_call x1, Pallas kernels, gather_tiles(): pl.pallas_call(gather_kernel, out_shape=jax.ShapeDtypeStruct((4, 4, 4, RO...  86.9 us
  transfers between devices with their start and end apart: 5, of which 3 were waited for; matrix products, arithmetic and copies ran while one was open for 4% of the time, Pallas kernels for 19%

profile of v2, /device:TPU:1, one launch (start us, length us, event | category | flops | bytes accessed | tf_op | source)
XLA Modules:
  0.0 458.6 jit_solution(14032216304398197546)
XLA Ops:
  0.6 1.4 collective-permute-start
  2.1 0.9 slice.53
  3.0 8.5 %collective-permute-start.1 = (f32[35840]{0:T(1024)S(1)}, f32[35840]{0:T(1024)S(1)}, u32[]{:S(2)}, u32[]{:S(2)}) collective-permute-start(f32[35840]{0:T(1024)S(1)} %bitcast.91), channel_id=1, source_target_pairs={{0,127},{1,0},{2,1},{3,2},{4,3},{5,4},{6,5},{7,6},{8,7},{9,8},{10,... | collective-permute-start | bytes 430088 | tf_op jit(solution)/shard_map/ppermute | solution.py:436
  11.5 2.0 reduce
  13.5 1.3 slice_bitcast_fusion.1.gain_src
  14.8 0.0 collective-permute-done.1
  14.8 2.5 concatenate.16
  17.3 1.0 dynamic-slice
  18.3 1.0 dynamic_slice.9
  19.3 86.9 %gather_tiles.1 = bf16[4,4,4,800,128]{4,3,2,1,0:T(8,128)(2,1)} custom-call(f32[24,38,1,128]{3,2,1,0:T(1,128)} %bitcast.87, f32[120,7,1,128]{3,2,1,0:T(1,128)} %bitcast.88, f32[1,8,1,128]{3,2,1,0:T(1,128)} %slice_bitcast_fusion.1.gain_src), custom_call_target="tpu_custom_call" | custom-call | tf_op jit(solution)/shard_map/gather_tiles/pallas_call | solution.py:192
  106.2 0.7 fusion.7
  106.9 0.0 copy-start
  106.9 7.6 %fusion.16 = (bf16[2128,8,128]{2,1,0:T(8,128)(2,1)S(1)}, bf16[2128,8,128]{2,1,0:T(8,128)(2,1)}, bf16[2128,8,128]{2,1,0:T(8,128)(2,1)S(1)}) fusion(bf16[6400,8,128]{2,1,0:T(8,128)(2,1)} %bitcast.69), kind=kLoop, calls=%fused_computation.42 | loop fusion | bytes 26148864 | tf_op jit(solution)/shard_map/slice | solution.py:462
  114.4 0.0 copy-start.2
  114.4 0.0 copy-start.1
  114.4 0.0 collective-permute-done
  114.5 0.0 copy-done
  114.5 3.7 multiply_reduce_fusion.1
  118.2 16.4 %fusion.14 = f32[2048,2432]{1,0:T(8,128)} fusion(bf16[896,2432]{1,0:T(8,128)(2,1)S(1)} %bitcast.83, f32[896]{0:T(1024)S(1)} %fusion.7, f32[2048]{0:T(1024)S(1)} %add_rsqrt_fusion, bf16[1024,896]{1,0:T(8,128)(2,1)} %collective-permute-done, bf16[1024,896]{1,0:T(8,128)(2,1)S(1)} %bitcast.75), kind=kOutput, calls=%fused_computation.41 | convolution fusion | flops 8938323968 | bytes 27962880 | tf_op jit(solution)/shard_map/dot_general | solution.py:430
  134.6 0.0 copy-done.2
  134.6 0.0 copy-done.1
  134.6 24.5 %multiply_convert_fusion.2 = (bf16[2048,2432]{1,0:T(8,128)(2,1)}, f32[2048,2432]{1,0:T(8,128)}) fusion(f32[2048,2432]{1,0:T(8,128)} %fusion.14, bf16[896,2432]{1,0:T(8,128)(2,1)S(1)} %bitcast.81, f32[896]{0:T(1024)S(1)} %fusion.7, f32[2048]{0:T(1024)S(1)} %add_rsqrt_fusion, bf16[1024,896]{1,0:T(8,128)(2,1)} %collective-permute-done, ...), kind=kOutput, calls=%fused_computation.2 | convolution fusion | flops 8968208384 | bytes 57847296 | tf_op jit(solution)/shard_map/dot_general | solution.py:430
  159.1 15.1 %fusion.17 = f32[2048,896]{1,0:T(8,128)S(1)} fusion(bf16[2048,2432]{1,0:T(8,128)(2,1)} %get-tuple-element.22, bf16[2432,896]{1,0:T(8,128)(2,1)} %bitcast.85), kind=kOutput, calls=%fused_computation.43 | convolution fusion | flops 8925478912 | bytes 21659648 | tf_op jit(solution)/shard_map/dot_general | solution.py:430
  174.2 0.2 slice.75
  174.4 0.0 copy-start.4
  174.5 4.5 collective-permute-start.2
  179.0 2.0 fusion.10
  180.9 4.1 collective-permute-done.2
  185.0 0.0 copy-done.4
  185.0 5.2 %multiply_reduce_fusion.2 = (f32[]{:T(128)}, bf16[1024,896]{1,0:T(8,128)(2,1)}) fusion(bf16[1,4,256,896]{3,2,1,0:T(8,128)(2,1)S(1)} %copy-done.4, f32[1024,896]{1,0:T(8,128)} %collective-permute-done.2, f32[2048,896]{1,0:T(8,128)S(1)} %fusion.17, f32[2048,896]{1,0:T(8,128)S(1)} %fusion.10), kind=kLoop, calls=%fused_computation.13 | loop fusion | flops 6422527 | bytes 14680068 | tf_op jit(solution)/shard_map/reduce_sum | solution.py:476
  190.2 0.3 collective-permute-start.3
  191.2 2.8 collective-permute-done.3
  193.9 26.5 %multiply_convert_fusion = (bf16[2048,2432]{1,0:T(8,128)(2,1)}, bf16[2048,2432]{1,0:T(8,128)(2,1)}) fusion(f32[2048,2432]{1,0:T(8,128)} %fusion.14, f32[2048,2432]{1,0:T(8,128)} %get-tuple-element.23, bf16[2432,896]{1,0:T(8,128)(2,1)} %bitcast.86, bf16[1024,896]{1,0:T(8,128)(2,1)} %collective-permute-done.3, bf16[1024,896]{1,0:T(8,128)(2,1)} %get-tuple-element.14), kind=kOutput, calls=%fused_computation | convolution fusion | flops 8997568512 | bytes 67796992 | tf_op jit(solution)/shard_map/dot_general | solution.py:430
  220.4 16.2 %fusion.18 = f32[2048,896]{1,0:T(8,128)} fusion(bf16[2048,2432]{1,0:T(8,128)(2,1)} %get-tuple-element.16, bf16[896,2432]{1,0:T(8,128)(2,1)} %bitcast.84), kind=kOutput, calls=%fused_computation.44 | convolution fusion | flops 8925478912 | bytes 21659648 | tf_op jit(solution)/shard_map/dot_general | solution.py:430
  236.6 0.0 slice-start.3
  236.6 0.0 slice-start.4
  236.6 17.2 %multiply_reduce_fusion = f32[896]{0:T(1024)S(1)} fusion(f32[2048,896]{1,0:T(8,128)} %fusion.18, f32[2048]{0:T(1024)S(1)} %add_rsqrt_fusion, bf16[2048,2432]{1,0:T(8,128)(2,1)} %get-tuple-element.15, bf16[896,2432]{1,0:T(8,128)(2,1)} %bitcast.82, bf16[1024,896]{1,0:T(8,128)(2,1)} %collective-permute-done, bf16[1024,896]{1,0:T(8,128)(2,1)S(1)} %bitcast.78), kind=kOutput, calls=%fused_computation.5 | convolution fusion | flops 8940157952 | bytes 25341440 | tf_op jit(solution)/shard_map/dot_general | solution.py:430
  253.9 0.6 fusion.6.g_tail
  254.5 0.0 slice-start.5
  254.5 0.0 slice-start
  254.5 17.2 %fusion.3 = f32[2432,896]{1,0:T(8,128)} fusion(bf16[2048,2432]{1,0:T(8,128)(2,1)} %get-tuple-element.22, bf16[1024,896]{1,0:T(8,128)(2,1)} %collective-permute-done.3, bf16[1024,896]{1,0:T(8,128)(2,1)} %get-tuple-element.14), kind=kOutput, calls=%fused_computation.14 | convolution fusion | flops 8932818944 | bytes 22347776 | tf_op jit(solution)/shard_map/dot_general | solution.py:430
  271.8 0.0 slice-done.3
  271.8 0.0 slice-done.4
  271.8 0.0 slice-done.5
  271.8 0.0 slice-start.2
  271.8 14.0 %fusion.11 = f32[896,2432]{1,0:T(8,128)} fusion(bf16[2048,2432]{1,0:T(8,128)(2,1)S(1)} %bitcast.95, f32[896]{0:T(1024)S(1)} %fusion.7, f32[2048]{0:T(1024)S(1)} %add_rsqrt_fusion, bf16[1024,896]{1,0:T(8,128)(2,1)} %collective-permute-done, bf16[1024,896]{1,0:T(8,128)(2,1)S(1)} %bitcast.79), kind=kOutput, calls=%fused_computation.38 | convolution fusion | flops 8938323968 | bytes 22359552 | tf_op jit(solution)/shard_map/dot_general | solution.py:430
  285.8 0.0 slice-done
  285.8 0.0 slice-done.1
  285.8 0.0 slice-done.2
  285.9 14.1 %fusion.12 = f32[896,2432]{1,0:T(8,128)} fusion(bf16[2048,2432]{1,0:T(8,128)(2,1)S(1)} %bitcast.93, f32[896]{0:T(1024)S(1)} %fusion.7, f32[2048]{0:T(1024)S(1)} %add_rsqrt_fusion, bf16[1024,896]{1,0:T(8,128)(2,1)} %collective-permute-done, bf16[1024,896]{1,0:T(8,128)(2,1)S(1)} %bitcast.80), kind=kOutput, calls=%fused_computation.39 | convolution fusion | flops 8938323968 | bytes 22359552 | tf_op jit(solution)/shard_map/dot_general | solution.py:430
  300.0 139.7 %scatter_tiles.1 = (f32[24,38,1,128]{3,2,1,0:T(1,128)}, f32[120,7,1,128]{3,2,1,0:T(1,128)}, f32[2,8,128]{2,1,0:T(8,128)}) custom-call(f32[2128,8,128]{2,1,0:T(8,128)} %bitcast.72, f32[2128,8,128]{2,1,0:T(8,128)} %bitcast.71, f32[2128,8,128]{2,1,0:T(8,128)} %bitcast.70, f32[16,8,128]{2,1,0:T(8,128)} %fusion.6.g_tail), custom_call_target="tpu_custom_call" | custom-call | tf_op jit(solution)/shard_map/scatter_tiles/pallas_call | solution.py:378
  439.7 0.7 slice_add_fusion.1
  440.4 0.7 fusion.31
  441.1 1.2 pad_select_fusion
  442.3 0.1 pad_maximum_fusion.4
  442.4 0.1 dynamic_slice.10
  442.5 2.5 collective-permute-start.4
  445.0 0.5 slice.68
  446.2 7.6 %collective-permute-done.4 = f32[35840]{0:T(1024)S(1)} collective-permute-done((f32[35840]{0:T(1024)S(1)}, f32[35840]{0:T(1024)S(1)}, u32[]{:S(2)}, u32[]{:S(2)}) %collective-permute-start.4) | collective-permute-done | bytes 143392 | tf_op jit(solution)/shard_map/ppermute | solution.py:502
  453.8 0.2 multiply_multiply_fusion
  454.0 0.0 copy-done.3
  454.0 0.0 copy-done.5
  454.0 0.0 copy-done.6
  454.0 3.3 multiply_subtract_fusion
  (11 shorter events, 0.0 us)
Async XLA Ops:
  0.6 113.8 %collective-permute-start = (bf16[1024,896]{1,0:T(8,128)(2,1)}, bf16[1024,896]{1,0:T(8,128)(2,1)}, u32[]{:S(2)}, u32[]{:S(2)}) collective-permute-start(bf16[1024,896]{1,0:T(8,128)(2,1)} %bitcast.73), channel_id=1, source_target_pairs={{0,64},{64,0},{1,65},{65,1},{2,66},{66,2},{3,67},{67,3},{4,68},{68... | collective-permute-start | bytes 5505032 | tf_op jit(solution)/shard_map/ppermute | solution.py:465
  3.0 11.8 %collective-permute-start.1 = (f32[35840]{0:T(1024)S(1)}, f32[35840]{0:T(1024)S(1)}, u32[]{:S(2)}, u32[]{:S(2)}) collective-permute-start(f32[35840]{0:T(1024)S(1)} %bitcast.91), channel_id=1, source_target_pairs={{0,127},{1,0},{2,1},{3,2},{4,3},{5,4},{6,5},{7,6},{8,7},{9,8},{10,... | collective-permute-start | bytes 430088 | tf_op jit(solution)/shard_map/ppermute | solution.py:436
  106.9 7.6 %copy-start = (bf16[1,4,256,896]{3,2,1,0:T(8,128)(2,1)S(1)}, bf16[1,4,256,896]{3,2,1,0:T(8,128)(2,1)}, u32[]{:S(2)}) copy-start(bf16[1,4,256,896]{3,2,1,0:T(8,128)(2,1)} %param.8) | copy-start | bytes 5505028
  114.4 20.1 %copy-start.2 = (bf16[2128,8,128]{2,1,0:T(8,128)(2,1)}, bf16[2128,8,128]{2,1,0:T(8,128)(2,1)S(1)}, u32[]{:S(2)}) copy-start(bf16[2128,8,128]{2,1,0:T(8,128)(2,1)S(1)} %get-tuple-element.19) | copy-start | bytes 13074436
  114.4 20.1 %copy-start.1 = (bf16[2128,8,128]{2,1,0:T(8,128)(2,1)}, bf16[2128,8,128]{2,1,0:T(8,128)(2,1)S(1)}, u32[]{:S(2)}) copy-start(bf16[2128,8,128]{2,1,0:T(8,128)(2,1)S(1)} %get-tuple-element.17) | copy-start | bytes 13074436
  174.4 10.6 %copy-start.4 = (bf16[1,4,256,896]{3,2,1,0:T(8,128)(2,1)S(1)}, bf16[1,4,256,896]{3,2,1,0:T(8,128)(2,1)}, u32[]{:S(2)}) copy-start(bf16[1,4,256,896]{3,2,1,0:T(8,128)(2,1)} %param.9) | copy-start | bytes 5505028
  174.5 10.5 %collective-permute-start.2 = (f32[1024,896]{1,0:T(8,128)S(1)}, f32[1024,896]{1,0:T(8,128)}, u32[]{:S(2)}, u32[]{:S(2)}) collective-permute-start(f32[1024,896]{1,0:T(8,128)S(1)} %slice.75), channel_id=1, source_target_pairs={{0,64},{64,0},{1,65},{65,1},{2,66},{66,2},{3,67},{67,3},{4,68},{68... | collective-permute-start | bytes 11010056 | tf_op jit(solution)/shard_map/ppermute | solution.py:474
  190.2 3.7 collective-permute-start.3
  236.6 35.1 %slice-start.3 = ((s8[9961472]{0:T(1024)(128)(4,1)}), s8[1572864]{0:T(1024)(128)(4,1)S(1)}, s32[]{:S(2)}) async-start(s8[9961472]{0:T(1024)(128)(4,1)} %bitcast.94), calls=%async_computation.3 | async-start | bytes 3145728
  236.6 35.1 %slice-start.4 = ((s8[9961472]{0:T(1024)(128)(4,1)}), s8[4194304]{0:T(1024)(128)(4,1)S(1)}, s32[]{:S(2)}) async-start(s8[9961472]{0:T(1024)(128)(4,1)} %bitcast.94), calls=%async_computation.4 | async-start | bytes 8388608
  254.5 17.3 %slice-start.5 = ((s8[9961472]{0:T(1024)(128)(4,1)}), s8[4194304]{0:T(1024)(128)(4,1)S(1)}, s32[]{:S(2)}) async-start(s8[9961472]{0:T(1024)(128)(4,1)} %bitcast.94), calls=%async_computation.5 | async-start | bytes 8388608
  254.5 31.3 %slice-start = ((s8[9961472]{0:T(1024)(128)(4,1)}), s8[4194304]{0:T(1024)(128)(4,1)S(1)}, s32[]{:S(2)}) async-start(s8[9961472]{0:T(1024)(128)(4,1)} %bitcast.92), calls=%async_computation | async-start | bytes 8388608
  254.5 31.3 %slice-start.1 = ((s8[9961472]{0:T(1024)(128)(4,1)}), s8[4194304]{0:T(1024)(128)(4,1)S(1)}, s32[]{:S(2)}) async-start(s8[9961472]{0:T(1024)(128)(4,1)} %bitcast.92), calls=%async_computation.1 | async-start | bytes 8388608
  271.8 14.1 %slice-start.2 = ((s8[9961472]{0:T(1024)(128)(4,1)}), s8[1572864]{0:T(1024)(128)(4,1)S(1)}, s32[]{:S(2)}) async-start(s8[9961472]{0:T(1024)(128)(4,1)} %bitcast.92), calls=%async_computation.2 | async-start | bytes 3145728
  300.0 154.0 %copy-start.3 = (f32[1,102151]{1,0:T(1,128)S(1)}, f32[1,102151]{1,0:T(1,128)}, u32[]{:S(2)}) copy-start(f32[1,102151]{1,0:T(1,128)} %param.5) | copy-start | bytes 1225816
  300.0 154.0 %copy-start.5 = (f32[1,102151]{1,0:T(1,128)S(1)}, f32[1,102151]{1,0:T(1,128)}, u32[]{:S(2)}) copy-start(f32[1,102151]{1,0:T(1,128)} %param.6) | copy-start | bytes 1225816
  300.0 154.0 %copy-start.6 = (f32[1,102151]{1,0:T(1,128)S(1)}, f32[1,102151]{1,0:T(1,128)}, u32[]{:S(2)}) copy-start(f32[1,102151]{1,0:T(1,128)} %param.7) | copy-start | bytes 1225816
  442.5 11.2 %collective-permute-start.4 = (f32[35840]{0:T(1024)S(1)}, f32[35840]{0:T(1024)S(1)}, u32[]{:S(2)}, u32[]{:S(2)}) collective-permute-start(f32[35840]{0:T(1024)S(1)} %dynamic_slice.10), channel_id=1, source_target_pairs={{0,1},{1,2},{2,3},{3,4},{4,5},{5,6},{6,7},{7,8},{8,9},{9,10},{10,1... | collective-permute-start | bytes 430088 | tf_op jit(solution)/shard_map/ppermute | solution.py:502
